TPU v7x, 128 devices: a whole 4x4x4 slice. The times are simulated.
128 devices in a mesh: row: 16 (over y, x), col: 8 (over z, core).
Axes of the slice: x: 4, y: 4, z: 4, core: 2. Of those that a mesh axis runs over, the one named last changes fastest.
Arguments:
- trailing: float32 [16384, 16384], P('row', 'col'), may hold values from -36 to 36
- reflectors: float32 [4, 16384, 64], P(None, 'row'), may hold values from -0.046875 to 0.046875
Outputs:
- rotated: float32 [16384, 16384], P('row', 'col')
All inputs are finite; a program needn't handle non-finite values.
Results may differ from a plain program's by a relative error of at most 0.00015.
Values sent between devices are 32-bit elements; how exact they have to be, the bound alone decides.
A program may use at most 128 MiB of HBM per device.

v0:
```python
import jax
import jax.numpy as jnp
from jax import lax
from jax.sharding import PartitionSpec as P


def sent_to_all(array, axis):
    copies = jnp.broadcast_to(array, (lax.axis_size(axis), *array.shape))
    return lax.all_to_all(copies, axis, split_axis=0, concat_axis=0, tiled=True)


def over_copies(array, axis):
    return sent_to_all(array, axis).sum(axis=0)


def over_pieces(array, axis):
    return lax.all_gather(array, axis).sum(0)


def product(left, right):
    return jnp.dot(left, right, precision=lax.Precision.HIGHEST, preferred_element_type=jnp.float32)


def unit_lower(raw_panels, first_row):
    shape = raw_panels.shape
    widths = shape[2]
    global_row = first_row + lax.broadcasted_iota(jnp.int32, shape, 1)
    pivot_row = (lax.broadcasted_iota(jnp.int32, shape, 0) + 1) * widths + lax.broadcasted_iota(
        jnp.int32, shape, 2
    )
    ones_part = jnp.where(
        global_row == pivot_row, jnp.ones_like(raw_panels), jnp.zeros_like(raw_panels)
    )
    return jnp.where(global_row > pivot_row, raw_panels, ones_part)


def block_factor(gram_block):
    widths = gram_block.shape[0]
    row_ids = lax.broadcasted_iota(jnp.int32, (widths, widths), 0)
    col_ids = lax.broadcasted_iota(jnp.int32, (widths, widths), 1)
    identity = jnp.where(row_ids == col_ids, jnp.ones_like(gram_block), jnp.zeros_like(gram_block))
    halves = jnp.sum(gram_block * identity, axis=0) * 0.5
    strict = jnp.where(col_ids > row_ids, gram_block, jnp.zeros_like(gram_block))
    negated = -(strict / halves[None, :])
    inverse = identity + negated
    power = negated
    reach = 2
    while reach < widths:
        power = product(power, power)
        inverse = product(inverse, identity + power)
        reach = reach * 2
    return inverse / halves[:, None]


def local(trailing, reflectors):
    local_rows = trailing.shape[0]
    local_cols = trailing.shape[1]
    row_index = lax.axis_index("row")
    col_index = lax.axis_index("col")
    own_panels = unit_lower(reflectors, row_index * local_rows)
    gram_local = jnp.einsum("kin,kim->knm", own_panels, own_panels, precision=lax.Precision.HIGHEST)
    gram_all = over_copies(gram_local, "row")
    gathered = lax.all_gather(own_panels, "row", axis=1, tiled=True)
    column_panels = lax.dynamic_slice_in_dim(gathered, col_index * local_cols, local_cols, 1)
    matrix = trailing
    for step_index in range(reflectors.shape[0]):
        own_rows = own_panels[step_index]
        own_cols = column_panels[step_index]
        factor = block_factor(gram_all[step_index])
        partial_av = product(matrix, own_cols)
        summed = over_pieces(partial_av, "col")
        applied = product(summed, factor)
        inner_sum = over_copies(product(own_rows.T, applied), "row")
        coupling = product(factor.T, inner_sum)
        update_rows = applied - 0.5 * product(own_rows, coupling)
        whole_update = lax.all_gather(update_rows, "row", axis=0, tiled=True)
        update_cols = lax.dynamic_slice_in_dim(whole_update, col_index * local_cols, local_cols, 0)
        left_side = jnp.concatenate([own_rows, update_rows], axis=1)
        right_side = jnp.concatenate([update_cols, own_cols], axis=1)
        matrix = matrix - product(left_side, right_side.T)
    return matrix


def solution(mesh):
    placed = (P("row", "col"), P(None, "row", None))
    return jax.shard_map(
        local, mesh=mesh, in_specs=placed, out_specs=P("row", "col"), check_vma=False
    )
```

profile of v0, /device:TPU:0, one launch (start us, length us, event | category | flops | bytes accessed | tf_op | source)
XLA Modules:
  0.0 619.2 jit_solution(6899083745931883154)
XLA Ops:
  6.5 2.5 select_select_fusion
  9.1 114.0 %all-gather.14.cloned.1.call-done = f32[4,16384,64]{1,2,0:T(8,128)} async-done(((f32[4,1024,64]{1,2,0:T(8,128)}), f32[4,16384,64]{1,2,0:T(8,128)}) %all-gather.14.cloned.1.call-update) | async-done | bytes 16777232 | tf_op jit(solution)/shard_map/all_gather | solution.py:63
  123.1 2.7 dynamic-slice_bitcast_fusion
  125.8 0.8 copy-done.7
  126.6 11.1 %convolution_bitcast_fusion = f32[1024,64]{0,1:T(8,128)} fusion(f32[2048,64]{0,1:T(8,128)S(1)} %get-tuple-element.12, f32[1024,2048]{1,0:T(8,128)} %param.2), kind=kOutput, calls=%fused_computation.16 | convolution fusion | flops 1610612736 | bytes 9175040 | tf_op jit(solution)/shard_map/dot_general | solution.py:21
  137.8 1.1 fusion.178
  139.1 2.3 reshape.109
  141.4 22.5 %all_to_all.25 = f32[16,1,16384]{2,1,0:T(1,128)S(1)} all-to-all(f32[16,1,16384]{2,1,0:T(1,128)} %reshape.109), channel_id=1, replica_groups=mesh['row'=16,'col'=8] {'row'}, dimensions={0} | all-to-all | bytes 2097152 | tf_op jit(solution)/shard_map/all_to_all | solution.py:9
  163.9 0.5 broadcast.281
  164.4 4.3 reduce
  168.7 2.1 reshape.110
  172.8 2.8 copy.3
  175.5 0.5 bitcast_reduce_fusion.3
  176.1 0.4 fusion.182
  176.5 0.4 fusion.174
  176.9 0.3 reshape.111
  177.2 11.6 %all_to_all.26 = f32[16,1,4096]{2,1,0:T(1,128)S(1)} all-to-all(f32[16,1,4096]{2,1,0:T(1,128)S(1)} %reshape.111), channel_id=1, replica_groups=mesh['row'=16,'col'=8] {'row'}, dimensions={0} | all-to-all | bytes 524288 | tf_op jit(solution)/shard_map/all_to_all | solution.py:9
  188.9 1.2 reduce.1
  190.6 1.1 fusion.3
  191.7 0.6 all-gather.26.cloned.1.call-start
  192.4 48.3 %all-gather.16.cloned.1.call-done = f32[16384,64]{0,1:T(8,128)} async-done(((f32[1024,64]{0,1:T(8,128)}), f32[16384,64]{0,1:T(8,128)}) %all-gather.16.cloned.1.call-update) | async-done | bytes 4194320 | tf_op jit(solution)/shard_map/all_gather | solution.py:76
  240.7 1.1 constant_dynamic-slice_fusion.3
  241.8 9.7 %convolution_subtract_fusion.3 = f32[1024,2048]{1,0:T(8,128)S(1)} fusion(f32[1024,2048]{1,0:T(8,128)} %param.2, f32[2048,64]{0,1:T(8,128)S(1)} %copy-done.8, f32[2048,64]{0,1:T(8,128)S(1)} %constant_dynamic-slice_fusion.3, f32[1024,64]{0,1:T(8,128)} %fusion.3, f32[1024,64]{0,1:T(8,128)S(1)} %get-tuple-element.16), kind=kOutput, calls=%fused_computation.3 | convolution fusion | flops 3223715840 | bytes 18350080 | tf_op jit(solution)/shard_map/dot_general | solution.py:21
  251.6 3.4 copy-done.2
  255.0 9.0 %fusion.184 = f32[1024,64]{0,1:T(8,128)} fusion(f32[1024,2048]{1,0:T(8,128)S(1)} %convolution_subtract_fusion.3, f32[2048,64]{0,1:T(8,128)S(1)} %copy-done.6), kind=kOutput, calls=%fused_computation.252 | convolution fusion | flops 1610612736 | bytes 9175040 | tf_op jit(solution)/shard_map/dot_general | solution.py:21
  265.9 23.5 %all-gather.26.cloned.1.call-done = f32[8192,64]{0,1:T(8,128)} async-done(((f32[1024,64]{0,1:T(8,128)}), f32[8192,64]{0,1:T(8,128)}) %all-gather.26.cloned.1.call-update) | async-done | bytes 2097168 | tf_op jit(solution)/shard_map/all_gather | solution.py:17
  289.4 2.8 copy.4
  292.2 0.5 bitcast_reduce_fusion.2
  292.7 0.4 fusion.188
  293.2 0.4 fusion.175
  293.9 15.7 %all_to_all.27 = f32[16,1,4096]{2,1,0:T(1,128)S(1)} all-to-all(f32[16,1,4096]{2,1,0:T(1,128)S(1)} %reshape.113), channel_id=1, replica_groups=mesh['row'=16,'col'=8] {'row'}, dimensions={0} | all-to-all | bytes 524288 | tf_op jit(solution)/shard_map/all_to_all | solution.py:9
  309.6 1.2 reduce.2
  311.1 1.0 fusion.189
  312.1 1.1 fusion.2
  313.2 47.8 %all-gather.18.cloned.1.call-done = f32[16384,64]{0,1:T(8,128)} async-done(((f32[1024,64]{0,1:T(8,128)}), f32[16384,64]{0,1:T(8,128)}) %all-gather.18.cloned.1.call-update) | async-done | bytes 4194320 | tf_op jit(solution)/shard_map/all_gather | solution.py:76
  361.1 1.1 constant_dynamic-slice_fusion.2
  362.2 9.7 %convolution_subtract_fusion.2 = f32[1024,2048]{1,0:T(8,128)S(1)} fusion(f32[1024,2048]{1,0:T(8,128)} %copy-done.2, f32[2048,64]{0,1:T(8,128)S(1)} %copy-done.6, f32[2048,64]{0,1:T(8,128)S(1)} %constant_dynamic-slice_fusion.2, f32[1024,64]{0,1:T(8,128)} %fusion.2, f32[1024,64]{0,1:T(8,128)S(1)} %get-tuple-element.15), kind=kOutput, calls=%fused_computation.2 | convolution fusion | flops 3223715840 | bytes 18350080 | tf_op jit(solution)/shard_map/dot_general | solution.py:21
  371.9 3.4 copy-done.1
  375.3 9.0 %fusion.190 = f32[1024,64]{0,1:T(8,128)} fusion(f32[1024,2048]{1,0:T(8,128)S(1)} %convolution_subtract_fusion.2, f32[2048,64]{0,1:T(8,128)S(1)} %copy-done.5), kind=kOutput, calls=%fused_computation.258 | convolution fusion | flops 1610612736 | bytes 9175040 | tf_op jit(solution)/shard_map/dot_general | solution.py:21
  384.3 0.4 all-gather.20.cloned.1.call-start
  386.5 23.2 %all-gather.28.cloned.1.call-done = f32[8192,64]{0,1:T(8,128)} async-done(((f32[1024,64]{0,1:T(8,128)}), f32[8192,64]{0,1:T(8,128)}) %all-gather.28.cloned.1.call-update) | async-done | bytes 2097168 | tf_op jit(solution)/shard_map/all_gather | solution.py:17
  409.7 2.8 copy.5
  412.5 0.5 bitcast_reduce_fusion.1
  413.0 0.4 fusion.194
  413.5 0.4 fusion.176
  414.2 15.7 %all_to_all.28 = f32[16,1,4096]{2,1,0:T(1,128)S(1)} all-to-all(f32[16,1,4096]{2,1,0:T(1,128)S(1)} %reshape.115), channel_id=1, replica_groups=mesh['row'=16,'col'=8] {'row'}, dimensions={0} | all-to-all | bytes 524288 | tf_op jit(solution)/shard_map/all_to_all | solution.py:9
  429.9 1.2 reduce.3
  431.6 1.1 fusion.1
  432.8 47.8 %all-gather.20.cloned.1.call-done = f32[16384,64]{0,1:T(8,128)} async-done(((f32[1024,64]{0,1:T(8,128)}), f32[16384,64]{0,1:T(8,128)}) %all-gather.20.cloned.1.call-update) | async-done | bytes 4194320 | tf_op jit(solution)/shard_map/all_gather | solution.py:76
  480.6 1.1 constant_dynamic-slice_fusion.1
  481.7 9.7 %convolution_subtract_fusion.1 = f32[1024,2048]{1,0:T(8,128)S(1)} fusion(f32[1024,2048]{1,0:T(8,128)} %copy-done.1, f32[2048,64]{0,1:T(8,128)S(1)} %copy-done.5, f32[2048,64]{0,1:T(8,128)S(1)} %constant_dynamic-slice_fusion.1, f32[1024,64]{0,1:T(8,128)} %fusion.1, f32[1024,64]{0,1:T(8,128)S(1)} %get-tuple-element.14), kind=kOutput, calls=%fused_computation.1 | convolution fusion | flops 3223715840 | bytes 18350080 | tf_op jit(solution)/shard_map/dot_general | solution.py:21
  491.4 3.4 copy-done
  494.8 9.0 %fusion.196 = f32[1024,64]{0,1:T(8,128)} fusion(f32[1024,2048]{1,0:T(8,128)S(1)} %convolution_subtract_fusion.1, f32[2048,64]{0,1:T(8,128)S(1)} %copy-done.4), kind=kOutput, calls=%fused_computation.264 | convolution fusion | flops 1610612736 | bytes 9175040 | tf_op jit(solution)/shard_map/dot_general | solution.py:21
  505.8 23.5 %all-gather.30.cloned.1.call-done = f32[8192,64]{0,1:T(8,128)} async-done(((f32[1024,64]{0,1:T(8,128)}), f32[8192,64]{0,1:T(8,128)}) %all-gather.30.cloned.1.call-update) | async-done | bytes 2097168 | tf_op jit(solution)/shard_map/all_gather | solution.py:17
  529.3 2.8 copy.6
  532.1 0.5 bitcast_reduce_fusion
  532.6 0.4 fusion.200
  533.0 0.4 fusion.177
  533.8 15.7 %all_to_all.29 = f32[16,1,4096]{2,1,0:T(1,128)S(1)} all-to-all(f32[16,1,4096]{2,1,0:T(1,128)S(1)} %reshape.117), channel_id=1, replica_groups=mesh['row'=16,'col'=8] {'row'}, dimensions={0} | all-to-all | bytes 524288 | tf_op jit(solution)/shard_map/all_to_all | solution.py:9
  549.4 1.2 reduce.4
  551.1 1.1 fusion
  552.3 47.9 %all-gather.22.cloned.1.call-done = f32[16384,64]{0,1:T(8,128)} async-done(((f32[1024,64]{0,1:T(8,128)}), f32[16384,64]{0,1:T(8,128)}) %all-gather.22.cloned.1.call-update) | async-done | bytes 4194320 | tf_op jit(solution)/shard_map/all_gather | solution.py:76
  600.2 1.1 constant_dynamic-slice_fusion
  601.2 11.2 %convolution_subtract_fusion = f32[1024,2048]{1,0:T(8,128)} fusion(f32[1024,2048]{1,0:T(8,128)} %copy-done, f32[2048,64]{0,1:T(8,128)S(1)} %copy-done.4, f32[2048,64]{0,1:T(8,128)S(1)} %constant_dynamic-slice_fusion, f32[1024,64]{0,1:T(8,128)} %fusion, f32[1024,64]{0,1:T(8,128)S(1)} %get-tuple-element.13), kind=kOutput, calls=%fused_computation | convolution fusion | flops 3223715840 | bytes 18350080 | tf_op jit(solution)/shard_map/dot_general | solution.py:21
  (101 shorter events, 10.9 us)
Async XLA Ops:
  6.5 116.5 %all-gather.14.cloned.1.call-start = ((), (), s32[]{:S(2)}) async-start(), calls=%async_computation.5 | async-start | bytes 17825792 | tf_op jit(solution)/shard_map/all_gather | solution.py:63
  9.0 128.7 %copy-start.3 = (f32[4,1024,64]{1,2,0:T(8,128)S(1)}, f32[4,1024,64]{1,2,0:T(8,128)}, u32[]{:S(2)}) copy-start(f32[4,1024,64]{1,2,0:T(8,128)} %select_select_fusion) | copy-start | bytes 3145732
  9.0 163.7 %all-gather.24.cloned.1.call-start = ((), (), s32[]{:S(2)}) async-start(), calls=%async_computation.10 | async-start | bytes 2359296 | tf_op jit(solution)/shard_map/all_gather | solution.py:17
  125.8 0.8 copy-start.7
  137.7 103.0 %all-gather.16.cloned.1.call-start = ((), (), s32[]{:S(2)}) async-start(), calls=%async_computation.6 | async-start | bytes 4456448 | tf_op jit(solution)/shard_map/all_gather | solution.py:76
  171.2 70.6 %copy-start.8 = (f32[2048,64]{0,1:T(8,128)S(1)}, f32[2048,64]{0,1:T(8,128)}, u32[]{:S(2)}) copy-start(f32[2048,64]{0,1:T(8,128)} %copy-done.7) | copy-start | bytes 1572868
  191.7 97.7 %all-gather.26.cloned.1.call-start = ((), (), s32[]{:S(2)}) async-start(), calls=%async_computation.11 | async-start | bytes 2359296 | tf_op jit(solution)/shard_map/all_gather | solution.py:17
  241.8 13.2 %copy-start.6 = (f32[2048,64]{0,1:T(8,128)S(1)}, f32[2048,64]{0,1:T(8,128)}, u32[]{:S(2)}) copy-start(f32[2048,64]{0,1:T(8,128)} %get-tuple-element.11) | copy-start | bytes 1572868
  251.6 3.4 copy-start.2
  264.0 97.1 %all-gather.18.cloned.1.call-start = ((), (), s32[]{:S(2)}) async-start(), calls=%async_computation.7 | async-start | bytes 4456448 | tf_op jit(solution)/shard_map/all_gather | solution.py:76
  265.9 27.2 %copy-start.9 = (f32[64,64]{1,0:T(8,128)}, f32[64,64]{1,0:T(8,128)S(1)}, u32[]{:S(2)}) copy-start(f32[64,64]{1,0:T(8,128)S(1)} %convolution_divide_fusion.2) | copy-start | bytes 49156
  313.2 96.5 %all-gather.28.cloned.1.call-start = ((), (), s32[]{:S(2)}) async-start(), calls=%async_computation.12 | async-start | bytes 2359296 | tf_op jit(solution)/shard_map/all_gather | solution.py:17
  362.2 13.2 %copy-start.5 = (f32[2048,64]{0,1:T(8,128)S(1)}, f32[2048,64]{0,1:T(8,128)}, u32[]{:S(2)}) copy-start(f32[2048,64]{0,1:T(8,128)} %get-tuple-element.10) | copy-start | bytes 1572868
  371.9 3.4 copy-start.1
  384.3 96.3 %all-gather.20.cloned.1.call-start = ((), (), s32[]{:S(2)}) async-start(), calls=%async_computation.8 | async-start | bytes 4456448 | tf_op jit(solution)/shard_map/all_gather | solution.py:76
  432.7 96.6 %all-gather.30.cloned.1.call-start = ((), (), s32[]{:S(2)}) async-start(), calls=%async_computation.13 | async-start | bytes 2359296 | tf_op jit(solution)/shard_map/all_gather | solution.py:17
  481.7 13.2 %copy-start.4 = (f32[2048,64]{0,1:T(8,128)S(1)}, f32[2048,64]{0,1:T(8,128)}, u32[]{:S(2)}) copy-start(f32[2048,64]{0,1:T(8,128)} %get-tuple-element.9) | copy-start | bytes 1572868
  491.4 3.4 copy-start
  503.8 96.3 %all-gather.22.cloned.1.call-start = ((), (), s32[]{:S(2)}) async-start(), calls=%async_computation.9 | async-start | bytes 4456448 | tf_op jit(solution)/shard_map/all_gather | solution.py:76
Sparse Core Ops, SparseCore 0:
  9.5 113.5 all-gather.13
  137.8 25.2 all-gather.23
  191.8 48.8 all-gather.15
  264.1 25.2 all-gather.25
  313.3 47.7 all-gather.17
  384.4 25.2 all-gather.27
  432.8 47.7 all-gather.19
  504.0 25.2 all-gather.29
  552.4 47.7 all-gather.21
where the time goes:
time: 625 us; the launch traced here: 619 us
  waiting for transfers between devices  376 us (60%)
  matrix products  95.4 us (15%)
  blocking collectives  81.2 us (13%)
  local copies, waits for them, and re-layouts  36.6 us (6%)
  between operations  14.1 us (2%)
  other arithmetic  14 us (2%)
    all_gather x4, waiting for transfers between devices, local(): whole_update = lax.all_gather(update_rows, 'row', axis=0, tiled=True)  192 us
    all_gather x1, waiting for transfers between devices, local(): gathered = lax.all_gather(own_panels, 'row', axis=1, tiled=True)  114 us
    dot_general x64, matrix products, product(): jnp.dot(left, right, precision=lax.Precision.HIGHEST, preferred_element_t...  94.3 us
    all_to_all x5, blocking collectives, sent_to_all(): return lax.all_to_all(copies, axis, split_axis=0, concat_axis=0, tiled=True)  81.2 us
    all_gather x4, waiting for transfers between devices, over_pieces(): return lax.all_gather(array, axis).sum(0)  70.2 us
    unnamed x34, local copies, waits for them, and re-layouts  28.6 us
  transfers between devices with their start and end apart: 9, of which 8 were waited for; matrix products, arithmetic and copies ran while one was open for 3% of the time, Pallas kernels for 0%

commit v1 on v0

v1 whole, which is shorter than its diff:
```python
import functools

import jax
import jax.numpy as jnp
from jax import lax
from jax.experimental import pallas as pl
from jax.experimental.pallas import tpu as pltpu
from jax.sharding import PartitionSpec as P

MESH = pl.DeviceIdType.MESH
F32 = jnp.float32
BF16 = jnp.bfloat16
DELTAS = (0, 1, 3, 2)


def exact(left, right, dims):
    return lax.dot_general(
        left, right, (dims, ((), ())), precision=lax.Precision.HIGHEST, preferred_element_type=F32
    )


def quick(left, right, dims):
    return lax.dot_general(left, right, (dims, ((), ())), preferred_element_type=F32)


def split(value):
    high = value.astype(BF16)
    low = (value - high.astype(F32)).astype(BF16)
    return high, low


NN = ((1,), (0,))
NT = ((1,), (1,))
TN = ((0,), (0,))


def unit_lower(raw_panels, first_row):
    shape = raw_panels.shape
    widths = shape[2]
    global_row = first_row + lax.broadcasted_iota(jnp.int32, shape, 1)
    pivot_row = (lax.broadcasted_iota(jnp.int32, shape, 0) + 1) * widths + lax.broadcasted_iota(
        jnp.int32, shape, 2
    )
    ones_part = jnp.where(
        global_row == pivot_row, jnp.ones_like(raw_panels), jnp.zeros_like(raw_panels)
    )
    return jnp.where(global_row > pivot_row, raw_panels, ones_part)


def exchange_kernel(
    a_hbm, v_ref,
    lhi_ref, llo_ref, rc_hbm,
    a_buf, a_hi, a_lo, vc, yc, yp, drx, yh, zrx, ys, yr,
    pb, xb, yb, gb, pw, inv, mm,
    a_sem, out_sem,
    t_send, t_recv, y_send, y_recv, x_send, x_recv,
    d_send, d_recv, zr_send, zr_recv, za_send, za_recv, e_send, e_recv,
    gx_send, gx_recv, gy_send, gy_recv, gg_send, gg_recv,
):
    row = lax.axis_index("row")
    col = lax.axis_index("col")
    x, y = row % 4, row // 4
    z, k = col // 2, col % 2

    def dev(dx, dy, dz, dk):
        return (dy * 4 + dx, dz * 2 + dk)

    def copy_to(src, dst, send, recv, device):
        return pltpu.make_async_remote_copy(
            src_ref=src, dst_ref=dst, send_sem=send, recv_sem=recv,
            device_id=device, device_id_type=MESH,
        )

    def arrived(dst, recv):
        copy_to(dst, dst, recv, recv, dev(x, y, z, 1 - k)).wait_recv()

    sent = []

    def send(copy, cond=None):
        if cond is None:
            copy.start()
        else:
            pl.when(cond)(copy.start)
        sent.append((copy, cond))

    is_src = k == x // 2
    b_own = x % 2
    stays = jnp.logical_and(y == z, is_src)

    def slab(i):
        return pltpu.make_async_copy(
            a_hbm.at[:, pl.ds(i * 256, 256)], a_buf.at[i], a_sem.at[i]
        )

    for i in range(8):
        slab(i).start()

    barrier = pltpu.get_barrier_semaphore()

    def greet(device):
        pl.semaphore_signal(barrier, inc=1, device_id=device, device_id_type=MESH)

    for d in range(1, 4):
        greet(dev((x + d) % 4, y, z, k))
        greet(dev(x, (y + d) % 4, z, k))
    for d in range(1, 8):
        greet((row, (col + d) % 8))

    @pl.when(y != z)
    def _():
        greet(dev(x, z, y, 0))
        greet(dev(x, z, y, 1))

    pl.semaphore_wait(barrier, jnp.where(y != z, 15, 13))

    def t_start(ph, q):
        target = vc if ph == 0 else yc
        source = v_ref.at[q, z, k] if ph == 0 else ys.at[q]
        place = target.at[q, b_own, z, k]
        send(
            copy_to(source, place, t_send.at[ph, q], t_recv.at[ph, q, k], dev(x, z, y, x // 2)),
            jnp.logical_not(stays),
        )

        @pl.when(stays)
        def _():
            if ph == 0:
                vc[q, b_own, z, k] = v_ref[q, z, k]
            else:
                yc[q, b_own, z, k] = ys[q]

    def y_start(ph, q):
        target = vc if ph == 0 else yc

        @pl.when(is_src)
        def _():
            for h in range(2):
                @pl.when(jnp.logical_not(jnp.logical_and(y == z, k == h)))
                def _():
                    arrived(target.at[q, b_own, y, h], t_recv.at[ph, q, h])

        unit = target.at[q, b_own, y]
        for d in range(1, 4):
            send(
                copy_to(unit, unit, y_send.at[ph, q, d - 1], y_recv.at[ph, q, y],
                        dev(x, (y + d) % 4, z, k)),
                is_src,
            )

    def x_own(ph, q, delta):
        target = vc if ph == 0 else yc
        j = (y + 4 - delta) % 4
        unit = target.at[q, b_own, j]
        if delta:
            @pl.when(is_src)
            def _():
                arrived(unit, y_recv.at[ph, q, j])
        for s, step in enumerate((1, 3)):
            send(
                copy_to(unit, unit, x_send.at[ph, q, 0, delta, s], x_recv.at[ph, q, b_own, j],
                        dev((x + step) % 4, y, z, k)),
                is_src,
            )

    def x_take(ph, q, delta, b):
        target = vc if ph == 0 else yc
        j = (y + 4 - delta) % 4
        far = (x + 4 - (2 * k + b)) % 4
        unit = target.at[q, b, j]

        @pl.when(far != 0)
        def _():
            arrived(unit, x_recv.at[ph, q, b, j])

        onward = 1 if delta in (0, 3) else 3
        send(
            copy_to(unit, unit, x_send.at[ph, q, 1 + b, delta, 0], x_recv.at[ph, q, b, j],
                    dev((x + onward) % 4, y, z, k)),
            far == onward,
        )

    def multiply(q, delta, b):
        j = (y + 4 - delta) % 4
        high, low = split(vc[q, b, j].reshape(256, 128))
        both = jnp.concatenate([high, low], axis=1)
        first = delta == 0 and b == 0

        def tile(m, carry):
            rows = pl.ds(pl.multiple_of(m * 256, 256), 256)
            wide = quick(a_hi[b * 4 + j, rows], both, NN)
            part = wide[:, :128] + wide[:, 128:] + quick(a_lo[b * 4 + j, rows], high, NN)
            part = part.reshape(2, 128, 128)
            if first:
                yp[q, m] = part
            else:
                yp[q, m] = yp[q, m] + part
            return carry

        lax.fori_loop(0, 4, tile, 0)

    def pair_start(q):
        send(copy_to(yp.at[q, :, 1 - k], drx.at[q], d_send.at[q], d_recv.at[q],
                     dev(x, y, z, 1 - k)))

    def scatter_start(q):
        arrived(drx.at[q], d_recv.at[q])
        yh[q] = yp[q, :, k] + drx[q]
        for d in range(1, 4):
            other = (z + d) % 4
            send(copy_to(yh.at[q, other], zrx.at[q, z], zr_send.at[q, d - 1], zr_recv.at[q, z],
                         dev(x, y, other, k)))
        zrx[q, z] = yh[q, z]

    def scatter_finish(q):
        for d in range(1, 4):
            other = (z + d) % 4
            arrived(zrx.at[q, other], zr_recv.at[q, other])
        total = zrx[q, 0] + zrx[q, 1] + zrx[q, 2] + zrx[q, 3]
        ys[q] = total
        yr[q, z, k] = total
        t_start(1, q)
        for d in range(1, 4):
            send(copy_to(ys.at[q], yr.at[q, z, k], za_send.at[q, d - 1], za_recv.at[q, z],
                         dev(x, y, (z + d) % 4, k)))

    def rows_pass(q):
        for d in range(1, 4):
            other = (z + d) % 4
            arrived(yr.at[q, other, k], za_recv.at[q, other])
        half = yr.at[q, :, k]
        send(copy_to(half, half, e_send.at[q], e_recv.at[q], dev(x, y, z, 1 - k)))

    def rows_finish(q):
        arrived(yr.at[q, :, 1 - k], e_recv.at[q])

    def sum_start(g):
        for d in range(1, 4):
            send(copy_to(pb.at[g, col], xb.at[g, x], gx_send.at[g, d - 1], gx_recv.at[g, x],
                         dev((x + d) % 4, y, z, k)))
        xb[g, x] = pb[g, col]

    def sum_middle(g):
        for d in range(1, 4):
            other = (x + d) % 4
            arrived(xb.at[g, other], gx_recv.at[g, other])
        yb[g, y] = xb[g, 0] + xb[g, 1] + xb[g, 2] + xb[g, 3]
        for d in range(1, 4):
            send(copy_to(yb.at[g, y], yb.at[g, y], gy_send.at[g, d - 1], gy_recv.at[g, y],
                         dev(x, (y + d) % 4, z, k)))

    def sum_gather(g):
        for d in range(1, 4):
            other = (y + d) % 4
            arrived(yb.at[g, other], gy_recv.at[g, other])
        gb[g, col] = yb[g, 0] + yb[g, 1] + yb[g, 2] + yb[g, 3]
        for d in range(1, 8):
            send(copy_to(gb.at[g, col], gb.at[g, col], gg_send.at[g, d - 1], gg_recv.at[g, col],
                         (row, (col + d) % 8)))

    def sum_finish(g):
        for d in range(1, 8):
            other = (col + d) % 8
            arrived(gb.at[g, other], gg_recv.at[g, other])

    def own_rows(ref, j):
        return jnp.concatenate(
            [ref[0, j].reshape(256, 128), ref[1, j].reshape(256, 128)], axis=1
        )

    def inner(g, right_ref):
        def part(j, carry):
            piece = exact(own_rows(v_ref, j), own_rows(right_ref, j), TN).reshape(8, 32, 256)

            @pl.when(j == 0)
            def _():
                pb[g] = piece

            @pl.when(j > 0)
            def _():
                pb[g] = pb[g] + piece

            return carry

        lax.fori_loop(0, 4, part, 0)

    ri = lax.broadcasted_iota(jnp.int32, (256, 256), 0)
    ci = lax.broadcasted_iota(jnp.int32, (256, 256), 1)

    def eye():
        return jnp.where(ri == ci, 1.0, 0.0).astype(F32)

    def factor_start():
        gram = gb[0].reshape(256, 256)
        halves = jnp.sum(jnp.where(ri == ci, gram, 0.0), axis=0, keepdims=True) * 0.5
        block = jnp.logical_and(ri // 64 == ci // 64, ci > ri)
        negated = -(jnp.where(block, gram, 0.0) / halves)
        pw[...] = negated
        inv[...] = eye() + negated

    def factor_double():
        power = exact(pw[...], pw[...], NN)
        pw[...] = power
        inv[...] = exact(inv[...], eye() + power, NN)

    def factor_scale():
        gram = gb[0].reshape(256, 256)
        halves = jnp.sum(jnp.where(ri == ci, gram, 0.0), axis=1, keepdims=True) * 0.5
        inv[...] = inv[...] / halves

    def factor_join(width):
        gram = gb[0].reshape(256, 256)
        above = jnp.logical_and(ri // (2 * width) == ci // (2 * width), ri // width < ci // width)
        off = jnp.where(above, gram, 0.0)
        inv[...] = inv[...] - exact(exact(inv[...], off, NN), inv[...], NN)

    def write_out(plane, source, q):
        copies = []
        for b in range(2):
            copies.append(pltpu.make_async_copy(
                source.at[q, b], rc_hbm.at[plane, b], out_sem.at[plane, b]))
        for copy in copies:
            copy.start()
        return copies

    t_start(0, 0)
    t_start(0, 1)
    inner(0, v_ref)
    sum_start(0)

    for i in range(8):
        slab(i).wait()

        def chop(m, carry):
            rows = pl.ds(pl.multiple_of(m * 128, 128), 128)
            high, low = split(a_buf[i, rows])
            a_hi[i, rows] = high
            a_lo[i, rows] = low
            return carry

        lax.fori_loop(0, 8, chop, 0)
        if i == 3:
            y_start(0, 0)
            x_own(0, 0, 0)
            y_start(0, 1)
    sum_middle(0)
    for delta in DELTAS[1:]:
        x_own(0, 0, delta)
    sum_gather(0)
    for delta in DELTAS:
        for b in range(2):
            x_take(0, 0, delta, b)
        x_own(0, 1, delta)
        for b in range(2):
            multiply(0, delta, b)
    pair_start(0)
    for n, delta in enumerate(DELTAS):
        for b in range(2):
            x_take(0, 1, delta, b)
        if n == 0:
            scatter_start(0)
        for b in range(2):
            multiply(1, delta, b)
        if n == 2:
            scatter_finish(0)
    pair_start(1)
    out_copies = write_out(2, vc, 0) + write_out(3, vc, 1)
    y_start(1, 0)
    x_own(1, 0, 0)
    scatter_start(1)
    for delta in DELTAS[1:]:
        x_own(1, 0, delta)
    sum_finish(0)
    factor_start()
    factor_double()
    scatter_finish(1)
    for n, delta in enumerate(DELTAS):
        for b in range(2):
            x_take(1, 0, delta, b)
        if n == 0:
            y_start(1, 1)
            rows_pass(0)
            rows_pass(1)
        x_own(1, 1, delta)
        if n == 1:
            rows_finish(0)
            rows_finish(1)
            inner(1, yr)
            sum_start(1)
        else:
            factor_double()
        if n == 2:
            sum_middle(1)
        if n == 3:
            sum_gather(1)
    out_copies += write_out(0, yc, 0)
    for n, delta in enumerate(DELTAS):
        for b in range(2):
            x_take(1, 1, delta, b)
        if n == 0:
            factor_double()
            factor_scale()
            factor_join(64)
            factor_join(128)
        if n == 1:
            sum_finish(1)
            moved = exact(gb[1].reshape(256, 256), inv[...], NN)
            mm[...] = exact(inv[...], moved, TN)
        if n == 2:
            def left(j, carry):
                rows = pl.ds(pl.multiple_of(j * 256, 256), 256)
                v_rows = own_rows(v_ref, j)
                high, low = split(exact(v_rows, inv[...], NT))
                lhi_ref[rows, :256] = high
                llo_ref[rows, :256] = low
                other = exact(own_rows(yr, j), inv[...], NN) - exact(v_rows, mm[...], NN)
                high, low = split(other)
                lhi_ref[rows, 256:] = high
                llo_ref[rows, 256:] = low
                return carry

            lax.fori_loop(0, 4, left, 0)
    out_copies += write_out(1, yc, 1)

    for copy, cond in sent:
        if cond is None:
            copy.wait_send()
        else:
            pl.when(cond)(copy.wait_send)
    for copy in out_copies:
        copy.wait()


def exchange(trailing, panels):
    dma = pltpu.SemaphoreType.DMA
    return pl.pallas_call(
        exchange_kernel,
        out_shape=(
            jax.ShapeDtypeStruct((1024, 512), BF16),
            jax.ShapeDtypeStruct((1024, 512), BF16),
            jax.ShapeDtypeStruct((4, 2, 4, 2, 128, 128), F32),
        ),
        in_specs=[
            pl.BlockSpec(memory_space=pl.ANY),
            pl.BlockSpec(memory_space=pltpu.VMEM),
        ],
        out_specs=(
            pl.BlockSpec(memory_space=pltpu.VMEM),
            pl.BlockSpec(memory_space=pltpu.VMEM),
            pl.BlockSpec(memory_space=pl.ANY),
        ),
        scratch_shapes=[
            pltpu.VMEM((8, 1024, 256), F32),
            pltpu.VMEM((8, 1024, 256), BF16),
            pltpu.VMEM((8, 1024, 256), BF16),
            pltpu.VMEM((2, 2, 4, 2, 128, 128), F32),
            pltpu.VMEM((2, 2, 4, 2, 128, 128), F32),
            pltpu.VMEM((2, 4, 2, 128, 128), F32),
            pltpu.VMEM((2, 4, 128, 128), F32),
            pltpu.VMEM((2, 4, 128, 128), F32),
            pltpu.VMEM((2, 4, 128, 128), F32),
            pltpu.VMEM((2, 128, 128), F32),
            pltpu.VMEM((2, 4, 2, 128, 128), F32),
            pltpu.VMEM((2, 8, 32, 256), F32),
            pltpu.VMEM((2, 4, 32, 256), F32),
            pltpu.VMEM((2, 4, 32, 256), F32),
            pltpu.VMEM((2, 8, 32, 256), F32),
            pltpu.VMEM((256, 256), F32),
            pltpu.VMEM((256, 256), F32),
            pltpu.VMEM((256, 256), F32),
            dma((8,)),
            dma((4, 2)),
            dma((2, 2)),
            dma((2, 2, 2)),
            dma((2, 2, 3)),
            dma((2, 2, 4)),
            dma((2, 2, 3, 4, 2)),
            dma((2, 2, 2, 4)),
            dma((2,)),
            dma((2,)),
            dma((2, 3)),
            dma((2, 4)),
            dma((2, 3)),
            dma((2, 4)),
            dma((2,)),
            dma((2,)),
            dma((2, 3)),
            dma((2, 4)),
            dma((2, 3)),
            dma((2, 4)),
            dma((2, 7)),
            dma((2, 8)),
        ],
        compiler_params=pltpu.CompilerParams(
            collective_id=0, has_side_effects=True, vmem_limit_bytes=60 * 1024 * 1024
        ),
        cost_estimate=pl.CostEstimate(
            flops=4_000_000_000, bytes_accessed=16 * 1024 * 1024, transcendentals=0
        ),
        name="exchange",
    )(trailing, panels)


def update_kernel(a_ref, lhi_ref, llo_ref, r_ref, o_ref):
    right = jnp.concatenate([r_ref[n].reshape(256, 128) for n in range(4)], axis=1)
    high, low = split(right)

    def tile(m, carry):
        rows = pl.ds(pl.multiple_of(m * 256, 256), 256)
        left_high = lhi_ref[rows]
        part = quick(left_high, high, NT) + quick(left_high, low, NT)
        part = part + quick(llo_ref[rows], high, NT)
        o_ref[rows] = a_ref[rows] - part
        return carry

    lax.fori_loop(0, 4, tile, 0)


def update(trailing, left_high, left_low, right):
    return pl.pallas_call(
        update_kernel,
        grid=(8,),
        out_shape=jax.ShapeDtypeStruct(trailing.shape, F32),
        in_specs=[
            pl.BlockSpec((1024, 256), lambda i: (0, i)),
            pl.BlockSpec((1024, 512), lambda i: (0, 0)),
            pl.BlockSpec((1024, 512), lambda i: (0, 0)),
            pl.BlockSpec((4, 1, 1, 2, 128, 128), lambda i: (0, i // 4, i % 4, 0, 0, 0)),
        ],
        out_specs=pl.BlockSpec((1024, 256), lambda i: (0, i)),
        compiler_params=pltpu.CompilerParams(vmem_limit_bytes=40 * 1024 * 1024),
        name="update",
    )(trailing, left_high, left_low, right)


def local(trailing, reflectors):
    local_rows = trailing.shape[0]
    panels = unit_lower(reflectors, lax.axis_index("row") * local_rows)
    panels = jnp.concatenate([panels[0::2], panels[1::2]], axis=2)
    panels = panels.reshape(2, 4, 2, 128, 128)
    left_high, left_low, right = exchange(trailing, panels)
    return update(trailing, left_high, left_low, right)


def solution(mesh):
    placed = (P("row", "col"), P(None, "row", None))
    return jax.shard_map(
        local, mesh=mesh, in_specs=placed, out_specs=P("row", "col"), check_vma=False
    )
```

time: 625 us -> 161 us (0.26)
  the two profiles are of different devices: /device:TPU:0 before, /device:TPU:4 now
where the time goes in v1:
time: 161 us
  Pallas kernels  153 us (95%)
  local copies, waits for them, and re-layouts  6.01 us (4%)
    pallas_call x1, Pallas kernels, exchange(): pl.pallas_call(exchange_kernel, out_shape=(jax.ShapeDtypeStruct((1024, 51...  137 us
    pallas_call x1, Pallas kernels, update(): pl.pallas_call(update_kernel, grid=(8,), out_shape=jax.ShapeDtypeStruct(t...  16.4 us
    unnamed x6, local copies, waits for them, and re-layouts  4.63 us

profile of v1, /device:TPU:4, one launch (start us, length us, event | category | flops | bytes accessed | tf_op | source)
XLA Modules:
  0.0 160.9 jit_solution(8637541509941972827)
XLA Ops:
  0.0 1.5 select_select_fusion
  1.5 0.1 fusion.2
  1.6 0.1 pad_maximum_fusion
  1.7 1.3 copy.3
  3.0 136.9 %exchange.1 = (bf16[1024,512]{1,0:T(8,128)(2,1)}, bf16[1024,512]{1,0:T(8,128)(2,1)}, f32[4,2,4,2,128,128]{5,4,3,2,1,0:T(8,128)}) custom-call(f32[1024,2048]{1,0:T(8,128)} %a_ref.1, f32[2,4,2,128,128]{4,3,2,1,0:T(8,128)} %bitcast.1), custom_call_target="tpu_custom_call" | custom-call | flops 4000000000 | bytes 16777216 | tf_op jit(solution)/shard_map/exchange/pallas_call | solution.py:435
  140.0 0.0 copy-start
  140.0 2.2 %copy-done = f32[4,2,4,2,128,128]{5,4,3,2,1,0:T(8,128)S(1)} copy-done((f32[4,2,4,2,128,128]{5,4,3,2,1,0:T(8,128)S(1)}, f32[4,2,4,2,128,128]{5,4,3,2,1,0:T(8,128)}, u32[]{:S(2)}) %copy-start) | copy-done | bytes 4194328
  142.1 0.0 copy-start.1
  142.1 1.2 copy-done.1
  143.4 0.0 copy-start.2
  143.4 1.2 copy-done.2
  144.6 16.4 %update.1 = f32[1024,2048]{1,0:T(8,128)} custom-call(f32[1024,2048]{1,0:T(8,128)} %a_ref.1, bf16[1024,512]{1,0:T(8,128)(2,1)S(1)} %copy-done.1, bf16[1024,512]{1,0:T(8,128)(2,1)S(1)} %copy-done.2, f32[4,2,4,2,128,128]{5,4,3,2,1,0:T(8,128)S(1)} %copy-done), custom_call_target="tpu_custom_call" | custom-call | tf_op jit(solution)/shard_map/update/pallas_call | solution.py:519
  (2 shorter events, 0.0 us)
Async XLA Ops:
  140.0 2.2 %copy-start = (f32[4,2,4,2,128,128]{5,4,3,2,1,0:T(8,128)S(1)}, f32[4,2,4,2,128,128]{5,4,3,2,1,0:T(8,128)}, u32[]{:S(2)}) copy-start(f32[4,2,4,2,128,128]{5,4,3,2,1,0:T(8,128)} %get-tuple-element.10.r_ref) | copy-start | bytes 12582916
  142.1 1.2 copy-start.1
  143.4 1.2 copy-start.2

commit v2 on v1

v2 whole, which is shorter than its diff:
```python
import jax
import jax.numpy as jnp
from jax import lax
from jax.experimental import pallas as pl
from jax.experimental.pallas import tpu as pltpu
from jax.sharding import PartitionSpec as P

MESH = pl.DeviceIdType.MESH
F32 = jnp.float32
BF16 = jnp.bfloat16
TILE = 512


def exact(left, right, dims):
    return lax.dot_general(
        left, right, (dims, ((), ())), precision=lax.Precision.HIGHEST, preferred_element_type=F32
    )


def quick(left, right, dims):
    return lax.dot_general(left, right, (dims, ((), ())), preferred_element_type=F32)


def split(value):
    high = value.astype(BF16)
    low = (value - high.astype(F32)).astype(BF16)
    return high, low


NN = ((1,), (0,))
NT = ((1,), (1,))


def exchange_kernel(
    a_hbm, raw_ref,
    lhi_ref, llo_ref, rc_hbm,
    a_buf, a_hi, a_lo, vt, vr, vc, yc, yp, drx, yh, zrx, ys, yr,
    pb, xb, yb, gb, pw, inv, mm,
    a_sem, out_sem,
    t_send, t_recv, p_send, p_recv,
    d_send, d_recv, zr_send, zr_recv, za_send, za_recv, e_send, e_recv,
    gx_send, gx_recv, gy_send, gy_recv, gg_send, gg_recv,
):
    row = lax.axis_index("row")
    col = lax.axis_index("col")
    x, y = row % 4, row // 4
    z, k = col // 2, col % 2

    def dev(dx, dy, dz, dk):
        return (dy * 4 + dx, dz * 2 + dk)

    def copy_to(src, dst, send, recv, device):
        return pltpu.make_async_remote_copy(
            src_ref=src, dst_ref=dst, send_sem=send, recv_sem=recv,
            device_id=device, device_id_type=MESH,
        )

    def arrived(dst, recv):
        copy_to(dst, dst, recv, recv, dev(x, y, z, 1 - k)).wait_recv()

    sent = []

    def send(copy, cond=None):
        if cond is None:
            copy.start()
        else:
            pl.when(cond)(copy.start)
        sent.append((copy, cond))

    is_src = k == x // 2
    b_own = x % 2
    stays = jnp.logical_and(y == z, is_src)

    def slab(i):
        return pltpu.make_async_copy(
            a_hbm.at[:, pl.ds(i * 256, 256)], a_buf.at[i], a_sem.at[i]
        )

    for i in range(8):
        slab(i).start()

    barrier = pltpu.get_barrier_semaphore()

    def greet(device):
        pl.semaphore_signal(barrier, inc=1, device_id=device, device_id_type=MESH)

    for d in range(1, 4):
        greet(dev((x + d) % 4, y, z, k))
        greet(dev(x, (y + d) % 4, z, k))
    for d in range(1, 8):
        greet((row, (col + d) % 8))

    @pl.when(y != z)
    def _():
        greet(dev(x, z, y, 0))
        greet(dev(x, z, y, 1))

    for n in range(8):
        for q in range(2):
            piece = raw_ref[q * 128:(q + 1) * 128, n * 128:(n + 1) * 128]
            here = row * 1024 + n * 128 + lax.broadcasted_iota(jnp.int32, (128, 128), 1)
            pivot = (q * 128 + 64) + lax.broadcasted_iota(jnp.int32, (128, 128), 0)
            ones_part = jnp.where(here == pivot, 1.0, 0.0).astype(F32)
            piece = jnp.where(here > pivot, piece, ones_part)
            vt[q * 128:(q + 1) * 128, n * 128:(n + 1) * 128] = piece
            vr[q, n // 4, n % 4] = piece.T

    pl.semaphore_wait(barrier, jnp.where(y != z, 15, 13))

    def t_start(ph, q):
        target = vc if ph == 0 else yc
        source = vr.at[q, k, z] if ph == 0 else ys.at[q]
        place = target.at[q, b_own, k, z]
        send(
            copy_to(source, place, t_send.at[ph, q], t_recv.at[ph, q, k], dev(x, z, y, x // 2)),
            jnp.logical_not(stays),
        )

        @pl.when(stays)
        def _():
            if ph == 0:
                vc[q, b_own, k, z] = vr[q, k, z]
            else:
                yc[q, b_own, k, z] = ys[q]

    def spread(ph, q, slot, b, h, j, along_x, cond):
        piece = (vc if ph == 0 else yc).at[q, b, h, j]
        for d in range(1, 4):
            device = dev((x + d) % 4, y, z, k) if along_x else dev(x, (y + d) % 4, z, k)
            send(
                copy_to(piece, piece, p_send.at[ph, q, slot, d - 1], p_recv.at[ph, q, b, h, j],
                        device),
                cond,
            )

    def piece_in(ph, q, b, h, j, cond):
        @pl.when(cond)
        def _():
            arrived((vc if ph == 0 else yc).at[q, b, h, j], p_recv.at[ph, q, b, h, j])

    def step_a(ph, q):
        target = vc if ph == 0 else yc
        for h in range(2):
            @pl.when(jnp.logical_and(
                is_src, jnp.logical_not(jnp.logical_and(y == z, k == h))))
            def _():
                arrived(target.at[q, b_own, h, y], t_recv.at[ph, q, h])

            spread(ph, q, 2 * h, b_own, h, y, h == 1, is_src)
            spread(ph, q, 2 * h + 1, b_own, h, y, h == 0, is_src)

    def step_b(ph, q):
        for n, delta in enumerate((1, 3, 2)):
            j = (y + 4 - delta) % 4
            piece_in(ph, q, b_own, 0, j, is_src)
            spread(ph, q, 4 + n, b_own, 0, j, True, is_src)

    def foreign(b):
        return jnp.logical_not(jnp.logical_and(is_src, b_own == b))

    def step_c(ph, q):
        for b in range(2):
            piece_in(ph, q, b, 1, y, foreign(b))
            spread(ph, q, 7 + b, b, 1, y, False, foreign(b))

    def step_d(ph, q, b, h, jp):
        for j in (2 * jp, 2 * jp + 1):
            piece_in(ph, q, b, h, j, foreign(b) if h == 0 else y != j)

    def multiply(q, b, h, jp):
        high, low = split(vc[q, b, h, 2 * jp:2 * jp + 2].reshape(256, 128))
        both = jnp.concatenate([high, low], axis=1)
        i = b * 4 + h * 2 + jp

        def tile(m, carry):
            rows = pl.ds(pl.multiple_of(m * 256, 256), 256)
            wide = quick(a_hi[i, rows], both, NN)
            part = wide[:, :128] + wide[:, 128:] + quick(a_lo[i, rows], high, NN)
            part = part.reshape(2, 128, 128)
            place = (q, m // 2, pl.ds(2 * (m % 2), 2))
            if i == 0:
                yp[place] = part
            else:
                yp[place] = yp[place] + part
            return carry

        lax.fori_loop(0, 4, tile, 0)

    def pair_start(q):
        send(copy_to(yp.at[q, 1 - k], drx.at[q], d_send.at[q], d_recv.at[q],
                     dev(x, y, z, 1 - k)))

    def scatter_start(q):
        arrived(drx.at[q], d_recv.at[q])
        yh[q] = yp[q, k] + drx[q]
        for d in range(1, 4):
            other = (z + d) % 4
            send(copy_to(yh.at[q, other], zrx.at[q, z], zr_send.at[q, d - 1], zr_recv.at[q, z],
                         dev(x, y, other, k)))
        zrx[q, z] = yh[q, z]

    def scatter_finish(q):
        for d in range(1, 4):
            other = (z + d) % 4
            arrived(zrx.at[q, other], zr_recv.at[q, other])
        total = zrx[q, 0] + zrx[q, 1] + zrx[q, 2] + zrx[q, 3]
        ys[q] = total
        yr[q, k, z] = total
        t_start(1, q)
        for d in range(1, 4):
            send(copy_to(ys.at[q], yr.at[q, k, z], za_send.at[q, d - 1], za_recv.at[q, z],
                         dev(x, y, (z + d) % 4, k)))

    def rows_pass(q):
        for d in range(1, 4):
            other = (z + d) % 4
            arrived(yr.at[q, k, other], za_recv.at[q, other])
        half = yr.at[q, k]
        send(copy_to(half, half, e_send.at[q], e_recv.at[q], dev(x, y, z, 1 - k)))

    def rows_finish(q):
        arrived(yr.at[q, 1 - k], e_recv.at[q])

    def sum_start(g):
        for d in range(1, 4):
            send(copy_to(pb.at[g, col], xb.at[g, x], gx_send.at[g, d - 1], gx_recv.at[g, x],
                         dev((x + d) % 4, y, z, k)))
        xb[g, x] = pb[g, col]

    def sum_middle(g):
        for d in range(1, 4):
            other = (x + d) % 4
            arrived(xb.at[g, other], gx_recv.at[g, other])
        yb[g, y] = xb[g, 0] + xb[g, 1] + xb[g, 2] + xb[g, 3]
        for d in range(1, 4):
            send(copy_to(yb.at[g, y], yb.at[g, y], gy_send.at[g, d - 1], gy_recv.at[g, y],
                         dev(x, (y + d) % 4, z, k)))

    def sum_gather(g):
        for d in range(1, 4):
            other = (y + d) % 4
            arrived(yb.at[g, other], gy_recv.at[g, other])
        gb[g, col] = yb[g, 0] + yb[g, 1] + yb[g, 2] + yb[g, 3]
        for d in range(1, 8):
            send(copy_to(gb.at[g, col], gb.at[g, col], gg_send.at[g, d - 1], gg_recv.at[g, col],
                         (row, (col + d) % 8)))

    def sum_finish(g):
        for d in range(1, 8):
            other = (col + d) % 8
            arrived(gb.at[g, other], gg_recv.at[g, other])

    def own_rows(ref, m):
        here = (m // 2, pl.ds(2 * (m % 2), 2))
        return jnp.concatenate(
            [ref[(0,) + here].reshape(256, 128), ref[(1,) + here].reshape(256, 128)], axis=1
        )

    def inner(g, right_ref):
        def part(m, carry):
            left_part = vt[:, pl.ds(pl.multiple_of(m * 256, 256), 256)]
            piece = exact(left_part, own_rows(right_ref, m), NN).reshape(8, 32, 256)

            @pl.when(m == 0)
            def _():
                pb[g] = piece

            @pl.when(m > 0)
            def _():
                pb[g] = pb[g] + piece

            return carry

        lax.fori_loop(0, 4, part, 0)

    ri = lax.broadcasted_iota(jnp.int32, (256, 256), 0)
    ci = lax.broadcasted_iota(jnp.int32, (256, 256), 1)

    def eye():
        return jnp.where(ri == ci, 1.0, 0.0).astype(F32)

    def factor_start():
        gram = gb[0].reshape(256, 256)
        halves = jnp.sum(jnp.where(ri == ci, gram, 0.0), axis=0, keepdims=True) * 0.5
        block = jnp.logical_and(ri // 64 == ci // 64, ci > ri)
        negated = -(jnp.where(block, gram, 0.0) / halves)
        pw[...] = negated
        inv[...] = eye() + negated

    def factor_double(step, carry):
        power = exact(pw[...], pw[...], NN)
        pw[...] = power
        inv[...] = exact(inv[...], eye() + power, NN)
        return carry

    def factor_scale():
        gram = gb[0].reshape(256, 256)
        halves = jnp.sum(jnp.where(ri == ci, gram, 0.0), axis=1, keepdims=True) * 0.5
        inv[...] = inv[...] / halves

    def factor_join(width):
        gram = gb[0].reshape(256, 256)
        above = jnp.logical_and(ri // (2 * width) == ci // (2 * width), ri // width < ci // width)
        off = jnp.where(above, gram, 0.0)
        inv[...] = inv[...] - exact(exact(inv[...], off, NN), inv[...], NN)

    out_copies = []

    def write_out(plane, source, q, b, h):
        copy = pltpu.make_async_copy(
            source.at[q, b, h], rc_hbm.at[plane, b, h], out_sem.at[plane, b, h])
        copy.start()
        out_copies.append(copy)

    units = [(b, h, jp) for b in range(2) for h in range(2) for jp in range(2)]

    t_start(0, 0)
    t_start(0, 1)
    inner(0, vr)
    sum_start(0)
    step_a(0, 0)

    for i in range(8):
        slab(i).wait()

        def chop(m, carry):
            rows = pl.ds(pl.multiple_of(m * 128, 128), 128)
            high, low = split(a_buf[i, rows])
            a_hi[i, rows] = high
            a_lo[i, rows] = low
            return carry

        lax.fori_loop(0, 8, chop, 0)
    step_b(0, 0)
    step_c(0, 0)
    step_a(0, 1)
    sum_middle(0)
    for n, (b, h, jp) in enumerate(units):
        step_d(0, 0, b, h, jp)
        multiply(0, b, h, jp)
        if n == 1:
            step_b(0, 1)
            step_c(0, 1)
            sum_gather(0)
    pair_start(0)
    for n, (b, h, jp) in enumerate(units):
        step_d(0, 1, b, h, jp)
        multiply(1, b, h, jp)
        if n == 2:
            scatter_start(0)
        if n == 6:
            scatter_finish(0)
    pair_start(1)
    for q in range(2):
        for b in range(2):
            for h in range(2):
                write_out(2 + q, vc, q, b, h)
    step_a(1, 0)
    scatter_start(1)
    sum_finish(0)
    step_b(1, 0)
    step_c(1, 0)
    factor_start()
    scatter_finish(1)
    rows_pass(0)
    lax.fori_loop(0, 5, factor_double, 0)
    step_a(1, 1)
    rows_pass(1)
    factor_scale()
    factor_join(64)
    factor_join(128)
    rows_finish(0)
    rows_finish(1)
    step_b(1, 1)
    step_c(1, 1)
    inner(1, yr)
    sum_start(1)

    def left_panel(m, carry):
        rows = pl.ds(pl.multiple_of(m * 256, 256), 256)
        high, low = split(exact(own_rows(vr, m), inv[...], NT))
        lhi_ref[rows, :256] = high
        llo_ref[rows, :256] = low
        return carry

    lax.fori_loop(0, 4, left_panel, 0)
    sum_middle(1)
    for b, h, jp in units:
        step_d(1, 0, b, h, jp)
        if jp == 1:
            write_out(0, yc, 0, b, h)
    sum_gather(1)
    sum_finish(1)
    mm[...] = exact(inv[...].T, exact(gb[1].reshape(256, 256), inv[...], NN), NN)

    def left_update(m, carry):
        rows = pl.ds(pl.multiple_of(m * 256, 256), 256)
        other = exact(own_rows(yr, m), inv[...], NN) - exact(own_rows(vr, m), mm[...], NN)
        high, low = split(other)
        lhi_ref[rows, 256:] = high
        llo_ref[rows, 256:] = low
        return carry

    lax.fori_loop(0, 4, left_update, 0)
    for b, h, jp in units:
        step_d(1, 1, b, h, jp)
        if jp == 1:
            write_out(1, yc, 1, b, h)

    for copy, cond in sent:
        if cond is None:
            copy.wait_send()
        else:
            pl.when(cond)(copy.wait_send)
    for copy in out_copies:
        copy.wait()


def exchange(trailing, raw):
    dma = pltpu.SemaphoreType.DMA
    pieces = pltpu.VMEM((2, 2, 2, 4, 128, 128), F32)
    by_rows = pltpu.VMEM((2, 2, 4, 128, 128), F32)
    halves = pltpu.VMEM((2, 4, 128, 128), F32)
    whole = pltpu.VMEM((2, 8, 32, 256), F32)
    slices = pltpu.VMEM((2, 4, 32, 256), F32)
    square = pltpu.VMEM((256, 256), F32)
    return pl.pallas_call(
        exchange_kernel,
        out_shape=(
            jax.ShapeDtypeStruct((1024, 512), BF16),
            jax.ShapeDtypeStruct((1024, 512), BF16),
            jax.ShapeDtypeStruct((4, 2, 2, 4, 128, 128), F32),
        ),
        in_specs=[
            pl.BlockSpec(memory_space=pl.ANY),
            pl.BlockSpec(memory_space=pltpu.VMEM),
        ],
        out_specs=(
            pl.BlockSpec(memory_space=pltpu.VMEM),
            pl.BlockSpec(memory_space=pltpu.VMEM),
            pl.BlockSpec(memory_space=pl.ANY),
        ),
        scratch_shapes=[
            pltpu.VMEM((8, 1024, 256), F32),
            pltpu.VMEM((8, 1024, 256), BF16),
            pltpu.VMEM((8, 1024, 256), BF16),
            pltpu.VMEM((256, 1024), F32),
            by_rows, pieces, pieces, by_rows, halves, halves, halves,
            pltpu.VMEM((2, 128, 128), F32),
            by_rows, whole, slices, slices, whole, square, square, square,
            dma((8,)),
            dma((4, 2, 2)),
            dma((2, 2)),
            dma((2, 2, 2)),
            dma((2, 2, 9, 3)),
            dma((2, 2, 2, 2, 4)),
            dma((2,)),
            dma((2,)),
            dma((2, 3)),
            dma((2, 4)),
            dma((2, 3)),
            dma((2, 4)),
            dma((2,)),
            dma((2,)),
            dma((2, 3)),
            dma((2, 4)),
            dma((2, 3)),
            dma((2, 4)),
            dma((2, 7)),
            dma((2, 8)),
        ],
        compiler_params=pltpu.CompilerParams(
            collective_id=0, has_side_effects=True, vmem_limit_bytes=60 * 1024 * 1024
        ),
        cost_estimate=pl.CostEstimate(
            flops=4_000_000_000, bytes_accessed=16 * 1024 * 1024, transcendentals=0
        ),
        name="exchange",
    )(trailing, raw)


def update_kernel(a_ref, lhi_ref, llo_ref, r_ref, o_ref):
    right = jnp.concatenate([r_ref[n].reshape(256, 128) for n in range(4)], axis=1)
    high, low = split(right)
    right = jnp.concatenate([high, low, high], axis=1)

    def tile(m, carry):
        rows = pl.ds(pl.multiple_of(m * TILE, TILE), TILE)
        left_high = lhi_ref[rows]
        left = jnp.concatenate([left_high, left_high, llo_ref[rows]], axis=1)
        o_ref[rows] = a_ref[rows] - quick(left, right, NT)
        return carry

    lax.fori_loop(0, 1024 // TILE, tile, 0)


def update(trailing, left_high, left_low, right):
    return pl.pallas_call(
        update_kernel,
        grid=(8,),
        out_shape=jax.ShapeDtypeStruct(trailing.shape, F32),
        in_specs=[
            pl.BlockSpec((1024, 256), lambda i: (0, i)),
            pl.BlockSpec((1024, 512), lambda i: (0, 0)),
            pl.BlockSpec((1024, 512), lambda i: (0, 0)),
            pl.BlockSpec((4, 1, 1, 2, 128, 128), lambda i: (0, i // 4, i // 2 % 2, i % 2, 0, 0)),
        ],
        out_specs=pl.BlockSpec((1024, 256), lambda i: (0, i)),
        compiler_params=pltpu.CompilerParams(vmem_limit_bytes=62 * 1024 * 1024),
        name="update",
    )(trailing, left_high, left_low, right)


def local(trailing, reflectors):
    raw = jnp.swapaxes(reflectors, 1, 2).reshape(256, 1024)
    left_high, left_low, right = exchange(trailing, raw)
    return update(trailing, left_high, left_low, right)


def solution(mesh):
    placed = (P("row", "col"), P(None, "row", None))
    return jax.shard_map(
        local, mesh=mesh, in_specs=placed, out_specs=P("row", "col"), check_vma=False
    )
```

time: 161 us -> 110 us (0.68)
  the two profiles are of different devices: /device:TPU:4 before, /device:TPU:0 now
where the time goes in v2:
time: 110 us; the launch traced here: 109 us
  Pallas kernels  109 us (99%)
    pallas_call x1, Pallas kernels, exchange(): pl.pallas_call(exchange_kernel, out_shape=(jax.ShapeDtypeStruct((1024, 51...  93.6 us
    pallas_call x1, Pallas kernels, update(): pl.pallas_call(update_kernel, grid=(8,), out_shape=jax.ShapeDtypeStruct(t...  15.1 us

profile of v2, /device:TPU:0, one launch (start us, length us, event | category | flops | bytes accessed | tf_op | source)
XLA Modules:
  0.0 108.8 jit_solution(18430413041976357265)
XLA Ops:
  0.0 93.6 %exchange.1 = (bf16[1024,512]{1,0:T(8,128)(2,1)}, bf16[1024,512]{1,0:T(8,128)(2,1)}, f32[4,2,2,4,128,128]{5,4,3,2,1,0:T(8,128)}) custom-call(f32[1024,2048]{1,0:T(8,128)} %a_ref.1, f32[256,1024]{1,0:T(8,128)} %bitcast.3), custom_call_target="tpu_custom_call" | custom-call | flops 4000000000 | bytes 16777216 | tf_op jit(solution)/shard_map/exchange/pallas_call | solution.py:427
  93.7 15.1 %update.1 = f32[1024,2048]{1,0:T(8,128)} custom-call(f32[1024,2048]{1,0:T(8,128)} %a_ref.1, bf16[1024,512]{1,0:T(8,128)(2,1)} %get-tuple-element.8.lhi_ref, bf16[1024,512]{1,0:T(8,128)(2,1)} %get-tuple-element.9.llo_ref, f32[4,2,2,4,128,128]{5,4,3,2,1,0:T(8,128)} %get-tuple-element.10.r_ref), custom_call_target="tpu_custom_call" | custom-call | tf_op jit(solution)/shard_map/update/pallas_call | solution.py:498

commit v3 on v2

--- a/solution.py
+++ b/solution.py
@@ -8,7 +8,6 @@
 MESH = pl.DeviceIdType.MESH
 F32 = jnp.float32
 BF16 = jnp.bfloat16
-TILE = 512
 
 
 def exact(left, right, dims):
@@ -33,13 +32,13 @@
 
 def exchange_kernel(
     a_hbm, raw_ref,
-    lhi_ref, llo_ref, rc_hbm,
+    out_ref,
     a_buf, a_hi, a_lo, vt, vr, vc, yc, yp, drx, yh, zrx, ys, yr,
-    pb, xb, yb, gb, pw, inv, mm,
-    a_sem, out_sem,
+    pb, cb, xb, yb, gb, pw, inv, mm, lhi_ref, llo_ref,
+    a_sem,
     t_send, t_recv, p_send, p_recv,
     d_send, d_recv, zr_send, zr_recv, za_send, za_recv, e_send, e_recv,
-    gx_send, gx_recv, gy_send, gy_recv, gg_send, gg_recv,
+    gc_send, gc_recv, gx_send, gx_recv, gy_send, gy_recv, gg_send, gg_recv,
 ):
     row = lax.axis_index("row")
     col = lax.axis_index("col")
@@ -163,28 +162,30 @@
             piece_in(ph, q, b, 1, y, foreign(b))
             spread(ph, q, 7 + b, b, 1, y, False, foreign(b))
 
-    def step_d(ph, q, b, h, jp):
-        for j in (2 * jp, 2 * jp + 1):
-            piece_in(ph, q, b, h, j, foreign(b) if h == 0 else y != j)
-
-    def multiply(q, b, h, jp):
-        high, low = split(vc[q, b, h, 2 * jp:2 * jp + 2].reshape(256, 128))
+    def step_d(ph, q, b, h, j):
+        piece_in(ph, q, b, h, j, jnp.logical_or(
+            jnp.logical_and(h == 0, foreign(b)), jnp.logical_and(h == 1, y != j)))
+
+    def multiply(q, t):
+        b, h = (b_own + t // 2) % 2, t % 2
+        for j in range(4):
+            step_d(0, q, b, h, j)
+        high, low = split(vc[q, b, h].reshape(512, 128))
         both = jnp.concatenate([high, low], axis=1)
-        i = b * 4 + h * 2 + jp
+        i = b * 4 + h * 2
 
         def tile(m, carry):
-            rows = pl.ds(pl.multiple_of(m * 256, 256), 256)
-            wide = quick(a_hi[i, rows], both, NN)
-            part = wide[:, :128] + wide[:, 128:] + quick(a_lo[i, rows], high, NN)
-            part = part.reshape(2, 128, 128)
-            place = (q, m // 2, pl.ds(2 * (m % 2), 2))
-            if i == 0:
-                yp[place] = part
+            rows = pl.ds(pl.multiple_of(m * 512, 512), 512)
+            wide = quick(jnp.concatenate([a_hi[i, rows], a_hi[i + 1, rows]], axis=1), both, NN)
+            slim = quick(jnp.concatenate([a_lo[i, rows], a_lo[i + 1, rows]], axis=1), high, NN)
+            part = (wide[:, :128] + wide[:, 128:] + slim).reshape(4, 128, 128)
+            if t == 0:
+                yp[q, m] = part
             else:
-                yp[place] = yp[place] + part
+                yp[q, m] = yp[q, m] + part
             return carry
 
-        lax.fori_loop(0, 4, tile, 0)
+        lax.fori_loop(0, 2, tile, 0)
 
     def pair_start(q):
         send(copy_to(yp.at[q, 1 - k], drx.at[q], d_send.at[q], d_recv.at[q],
@@ -221,11 +222,26 @@
     def rows_finish(q):
         arrived(yr.at[q, 1 - k], e_recv.at[q])
 
+    def column_start():
+        for d in range(1, 8):
+            other = (col + d) % 8
+            send(copy_to(pb.at[1, other], cb.at[col], gc_send.at[d - 1], gc_recv.at[col],
+                         (row, other)))
+        cb[col] = pb[1, col]
+
+    def column_finish():
+        for d in range(1, 8):
+            other = (col + d) % 8
+            arrived(cb.at[other], gc_recv.at[other])
+        total = cb[0]
+        for n in range(1, 8):
+            total = total + cb[n]
+        xb[1, x] = total
+
     def sum_start(g):
         for d in range(1, 4):
-            send(copy_to(pb.at[g, col], xb.at[g, x], gx_send.at[g, d - 1], gx_recv.at[g, x],
+            send(copy_to(xb.at[g, x], xb.at[g, x], gx_send.at[g, d - 1], gx_recv.at[g, x],
                          dev((x + d) % 4, y, z, k)))
-        xb[g, x] = pb[g, col]
 
     def sum_middle(g):
         for d in range(1, 4):
@@ -304,19 +320,40 @@
         off = jnp.where(above, gram, 0.0)
         inv[...] = inv[...] - exact(exact(inv[...], off, NN), inv[...], NN)
 
-    out_copies = []
-
-    def write_out(plane, source, q, b, h):
-        copy = pltpu.make_async_copy(
-            source.at[q, b, h], rc_hbm.at[plane, b, h], out_sem.at[plane, b, h])
-        copy.start()
-        out_copies.append(copy)
-
-    units = [(b, h, jp) for b in range(2) for h in range(2) for jp in range(2)]
+    def place(t):
+        b, n = (b_own + t // 4) % 2, t % 4
+        h = (n + 1) // 2 % 2
+        jp = h * (n - 1) + (1 - h) * ((y // 2 + n // 3) % 2)
+        return b, h, jp
+
+    def finish(t, carry):
+        b, h, jp = place(t)
+        for q in range(2):
+            for n in range(2):
+                step_d(1, q, b, h, 2 * jp + n)
+        here = (b, h, pl.ds(2 * jp, 2))
+        right = jnp.concatenate(
+            [ref[(q,) + here].reshape(256, 128) for ref in (yc, vc) for q in range(2)], axis=1
+        )
+        high, low = split(right)
+        right = jnp.concatenate([high, low, high], axis=1)
+        i = b * 4 + h * 2 + jp
+
+        def tile(m, inside):
+            rows = pl.ds(pl.multiple_of(m * 512, 512), 512)
+            left_high = lhi_ref[rows]
+            left = jnp.concatenate([left_high, left_high, llo_ref[rows]], axis=1)
+            columns = pl.ds(pl.multiple_of(i * 256, 256), 256)
+            out_ref[rows, columns] = a_buf[i, rows] - quick(left, right, NT)
+            return inside
+
+        lax.fori_loop(0, 2, tile, 0)
+        return carry
 
     t_start(0, 0)
     t_start(0, 1)
     inner(0, vr)
+    xb[0, x] = pb[0, col]
     sum_start(0)
     step_a(0, 0)
 
@@ -335,46 +372,40 @@
     step_c(0, 0)
     step_a(0, 1)
     sum_middle(0)
-    for n, (b, h, jp) in enumerate(units):
-        step_d(0, 0, b, h, jp)
-        multiply(0, b, h, jp)
-        if n == 1:
+    for t in range(4):
+        multiply(0, t)
+        if t == 1:
             step_b(0, 1)
             step_c(0, 1)
             sum_gather(0)
     pair_start(0)
-    for n, (b, h, jp) in enumerate(units):
-        step_d(0, 1, b, h, jp)
-        multiply(1, b, h, jp)
-        if n == 2:
+    for t in range(4):
+        multiply(1, t)
+        if t == 0:
             scatter_start(0)
-        if n == 6:
+        if t == 2:
             scatter_finish(0)
     pair_start(1)
-    for q in range(2):
-        for b in range(2):
-            for h in range(2):
-                write_out(2 + q, vc, q, b, h)
+    inner(1, yp)
+    column_start()
     step_a(1, 0)
     scatter_start(1)
+    column_finish()
+    sum_start(1)
+    step_b(1, 0)
+    sum_middle(1)
+    step_c(1, 0)
+    scatter_finish(1)
     sum_finish(0)
-    step_b(1, 0)
-    step_c(1, 0)
     factor_start()
-    scatter_finish(1)
-    rows_pass(0)
     lax.fori_loop(0, 5, factor_double, 0)
-    step_a(1, 1)
-    rows_pass(1)
+    sum_gather(1)
     factor_scale()
     factor_join(64)
     factor_join(128)
-    rows_finish(0)
-    rows_finish(1)
-    step_b(1, 1)
-    step_c(1, 1)
-    inner(1, yr)
-    sum_start(1)
+    step_a(1, 1)
+    rows_pass(0)
+    rows_pass(1)
 
     def left_panel(m, carry):
         rows = pl.ds(pl.multiple_of(m * 256, 256), 256)
@@ -384,12 +415,10 @@
         return carry
 
     lax.fori_loop(0, 4, left_panel, 0)
-    sum_middle(1)
-    for b, h, jp in units:
-        step_d(1, 0, b, h, jp)
-        if jp == 1:
-            write_out(0, yc, 0, b, h)
-    sum_gather(1)
+    step_b(1, 1)
+    step_c(1, 1)
+    rows_finish(0)
+    rows_finish(1)
     sum_finish(1)
     mm[...] = exact(inv[...].T, exact(gb[1].reshape(256, 256), inv[...], NN), NN)
 
@@ -402,18 +431,13 @@
         return carry
 
     lax.fori_loop(0, 4, left_update, 0)
-    for b, h, jp in units:
-        step_d(1, 1, b, h, jp)
-        if jp == 1:
-            write_out(1, yc, 1, b, h)
+    lax.fori_loop(0, 8, finish, 0)
 
     for copy, cond in sent:
         if cond is None:
             copy.wait_send()
         else:
             pl.when(cond)(copy.wait_send)
-    for copy in out_copies:
-        copy.wait()
 
 
 def exchange(trailing, raw):
@@ -424,22 +448,15 @@
     whole = pltpu.VMEM((2, 8, 32, 256), F32)
     slices = pltpu.VMEM((2, 4, 32, 256), F32)
     square = pltpu.VMEM((256, 256), F32)
+    left = pltpu.VMEM((1024, 512), BF16)
     return pl.pallas_call(
         exchange_kernel,
-        out_shape=(
-            jax.ShapeDtypeStruct((1024, 512), BF16),
-            jax.ShapeDtypeStruct((1024, 512), BF16),
-            jax.ShapeDtypeStruct((4, 2, 2, 4, 128, 128), F32),
-        ),
+        out_shape=jax.ShapeDtypeStruct(trailing.shape, F32),
         in_specs=[
             pl.BlockSpec(memory_space=pl.ANY),
             pl.BlockSpec(memory_space=pltpu.VMEM),
         ],
-        out_specs=(
-            pl.BlockSpec(memory_space=pltpu.VMEM),
-            pl.BlockSpec(memory_space=pltpu.VMEM),
-            pl.BlockSpec(memory_space=pl.ANY),
-        ),
+        out_specs=pl.BlockSpec(memory_space=pltpu.VMEM),
         scratch_shapes=[
             pltpu.VMEM((8, 1024, 256), F32),
             pltpu.VMEM((8, 1024, 256), BF16),
@@ -447,9 +464,9 @@
             pltpu.VMEM((256, 1024), F32),
             by_rows, pieces, pieces, by_rows, halves, halves, halves,
             pltpu.VMEM((2, 128, 128), F32),
-            by_rows, whole, slices, slices, whole, square, square, square,
+            by_rows, whole, pltpu.VMEM((8, 32, 256), F32), slices, slices, whole,
+            square, square, square, left, left,
             dma((8,)),
-            dma((4, 2, 2)),
             dma((2, 2)),
             dma((2, 2, 2)),
             dma((2, 2, 9, 3)),
@@ -462,6 +479,8 @@
             dma((2, 4)),
             dma((2,)),
             dma((2,)),
+            dma((7,)),
+            dma((8,)),
             dma((2, 3)),
             dma((2, 4)),
             dma((2, 3)),
@@ -470,51 +489,18 @@
             dma((2, 8)),
         ],
         compiler_params=pltpu.CompilerParams(
-            collective_id=0, has_side_effects=True, vmem_limit_bytes=60 * 1024 * 1024
+            collective_id=0, has_side_effects=True, vmem_limit_bytes=44 * 1024 * 1024
         ),
         cost_estimate=pl.CostEstimate(
-            flops=4_000_000_000, bytes_accessed=16 * 1024 * 1024, transcendentals=0
+            flops=8_000_000_000, bytes_accessed=16 * 1024 * 1024, transcendentals=0
         ),
         name="exchange",
     )(trailing, raw)
 
 
-def update_kernel(a_ref, lhi_ref, llo_ref, r_ref, o_ref):
-    right = jnp.concatenate([r_ref[n].reshape(256, 128) for n in range(4)], axis=1)
-    high, low = split(right)
-    right = jnp.concatenate([high, low, high], axis=1)
-
-    def tile(m, carry):
-        rows = pl.ds(pl.multiple_of(m * TILE, TILE), TILE)
-        left_high = lhi_ref[rows]
-        left = jnp.concatenate([left_high, left_high, llo_ref[rows]], axis=1)
-        o_ref[rows] = a_ref[rows] - quick(left, right, NT)
-        return carry
-
-    lax.fori_loop(0, 1024 // TILE, tile, 0)
-
-
-def update(trailing, left_high, left_low, right):
-    return pl.pallas_call(
-        update_kernel,
-        grid=(8,),
-        out_shape=jax.ShapeDtypeStruct(trailing.shape, F32),
-        in_specs=[
-            pl.BlockSpec((1024, 256), lambda i: (0, i)),
-            pl.BlockSpec((1024, 512), lambda i: (0, 0)),
-            pl.BlockSpec((1024, 512), lambda i: (0, 0)),
-            pl.BlockSpec((4, 1, 1, 2, 128, 128), lambda i: (0, i // 4, i // 2 % 2, i % 2, 0, 0)),
-        ],
-        out_specs=pl.BlockSpec((1024, 256), lambda i: (0, i)),
-        compiler_params=pltpu.CompilerParams(vmem_limit_bytes=62 * 1024 * 1024),
-        name="update",
-    )(trailing, left_high, left_low, right)
-
-
 def local(trailing, reflectors):
     raw = jnp.swapaxes(reflectors, 1, 2).reshape(256, 1024)
-    left_high, left_low, right = exchange(trailing, raw)
-    return update(trailing, left_high, left_low, right)
+    return exchange(trailing, raw)
 
 
 def solution(mesh):

time: 110 us -> 95 us (0.86)
  the two profiles are of different devices: /device:TPU:0 before, /device:TPU:1 now
where the time goes in v3:
time: 95 us; the launch traced here: 94.9 us
  Pallas kernels  90.2 us (95%)
  local copies, waits for them, and re-layouts  4.62 us (5%)
    pallas_call x1, Pallas kernels, exchange(): pl.pallas_call(exchange_kernel, out_shape=jax.ShapeDtypeStruct(trailing.s...  90.2 us
    unnamed x3, local copies, waits for them, and re-layouts  4.62 us

profile of v3, /device:TPU:1, one launch (start us, length us, event | category | flops | bytes accessed | tf_op | source)
XLA Modules:
  0.0 94.9 jit_solution(14786233556855270118)
XLA Ops:
  0.0 0.0 copy-start
  0.0 1.2 %copy-done = f32[4,1024,64]{1,2,0:T(8,128)S(1)} copy-done((f32[4,1024,64]{1,2,0:T(8,128)S(1)}, f32[4,1024,64]{1,2,0:T(8,128)}, u32[]{:S(2)}) %copy-start) | copy-done | bytes 1048600
  1.2 90.2 %exchange.1 = f32[1024,2048]{1,0:T(8,128)S(1)} custom-call(f32[1024,2048]{1,0:T(8,128)} %a_hbm.1, f32[256,1024]{1,0:T(8,128)S(1)} %bitcast.3), custom_call_target="tpu_custom_call" | custom-call | flops 8000000000 | bytes 16777216 | tf_op jit(solution)/shard_map/exchange/pallas_call | solution.py:452
  91.5 3.4 %copy.4 = f32[1024,2048]{1,0:T(8,128)} copy(f32[1024,2048]{1,0:T(8,128)S(1)} %exchange.1) | data formatting | bytes 16777216
Async XLA Ops:
  0.0 1.2 %copy-start = (f32[4,1024,64]{1,2,0:T(8,128)S(1)}, f32[4,1024,64]{1,2,0:T(8,128)}, u32[]{:S(2)}) copy-start(f32[4,1024,64]{1,2,0:T(8,128)} %param.3) | copy-start | bytes 3145732

commit v4 on v3

--- a/solution.py
+++ b/solution.py
@@ -34,7 +34,7 @@
     a_hbm, raw_ref,
     out_ref,
     a_buf, a_hi, a_lo, vt, vr, vc, yc, yp, drx, yh, zrx, ys, yr,
-    pb, cb, xb, yb, gb, pw, inv, mm, lhi_ref, llo_ref,
+    pb, sb, cb, xb, yb, gb, pw, inv, mm, lhi_ref, llo_ref,
     a_sem,
     t_send, t_recv, p_send, p_recv,
     d_send, d_recv, zr_send, zr_recv, za_send, za_recv, e_send, e_recv,
@@ -222,21 +222,21 @@
     def rows_finish(q):
         arrived(yr.at[q, 1 - k], e_recv.at[q])
 
-    def column_start():
+    def column_start(q):
         for d in range(1, 8):
             other = (col + d) % 8
-            send(copy_to(pb.at[1, other], cb.at[col], gc_send.at[d - 1], gc_recv.at[col],
+            send(copy_to(sb.at[q, other], cb.at[q, col], gc_send.at[q, d - 1], gc_recv.at[q, col],
                          (row, other)))
-        cb[col] = pb[1, col]
-
-    def column_finish():
+        cb[q, col] = sb[q, col]
+
+    def column_finish(q):
         for d in range(1, 8):
             other = (col + d) % 8
-            arrived(cb.at[other], gc_recv.at[other])
-        total = cb[0]
+            arrived(cb.at[q, other], gc_recv.at[q, other])
+        total = cb[q, 0]
         for n in range(1, 8):
-            total = total + cb[n]
-        xb[1, x] = total
+            total = total + cb[q, n]
+        xb[1, x, :, q * 128:(q + 1) * 128] = total
 
     def sum_start(g):
         for d in range(1, 4):
@@ -272,22 +272,25 @@
             [ref[(0,) + here].reshape(256, 128), ref[(1,) + here].reshape(256, 128)], axis=1
         )
 
-    def inner(g, right_ref):
+    def inner(target, right_of):
         def part(m, carry):
             left_part = vt[:, pl.ds(pl.multiple_of(m * 256, 256), 256)]
-            piece = exact(left_part, own_rows(right_ref, m), NN).reshape(8, 32, 256)
+            piece = exact(left_part, right_of(m), NN).reshape(target.shape)
 
             @pl.when(m == 0)
             def _():
-                pb[g] = piece
+                target[...] = piece
 
             @pl.when(m > 0)
             def _():
-                pb[g] = pb[g] + piece
+                target[...] = target[...] + piece
 
             return carry
 
         lax.fori_loop(0, 4, part, 0)
+
+    def product_rows(q):
+        return lambda m: yp[q, m // 2, pl.ds(2 * (m % 2), 2)].reshape(256, 128)
 
     ri = lax.broadcasted_iota(jnp.int32, (256, 256), 0)
     ci = lax.broadcasted_iota(jnp.int32, (256, 256), 1)
@@ -352,8 +355,8 @@
 
     t_start(0, 0)
     t_start(0, 1)
-    inner(0, vr)
-    xb[0, x] = pb[0, col]
+    inner(pb, lambda m: own_rows(vr, m))
+    xb[0, x] = pb[col]
     sum_start(0)
     step_a(0, 0)
 
@@ -379,33 +382,33 @@
             step_c(0, 1)
             sum_gather(0)
     pair_start(0)
-    for t in range(4):
-        multiply(1, t)
-        if t == 0:
-            scatter_start(0)
-        if t == 2:
-            scatter_finish(0)
-    pair_start(1)
-    inner(1, yp)
-    column_start()
-    step_a(1, 0)
-    scatter_start(1)
-    column_finish()
-    sum_start(1)
-    step_b(1, 0)
-    sum_middle(1)
-    step_c(1, 0)
-    scatter_finish(1)
+    inner(sb.at[0], product_rows(0))
+    scatter_start(0)
+    column_start(0)
     sum_finish(0)
     factor_start()
     lax.fori_loop(0, 5, factor_double, 0)
-    sum_gather(1)
+    multiply(1, 0)
     factor_scale()
     factor_join(64)
     factor_join(128)
-    step_a(1, 1)
+    multiply(1, 1)
+    scatter_finish(0)
+    multiply(1, 2)
+    column_finish(0)
+    multiply(1, 3)
+    pair_start(1)
+    inner(sb.at[1], product_rows(1))
+    column_start(1)
+    scatter_start(1)
+    step_a(1, 0)
+    column_finish(1)
+    sum_start(1)
+    step_b(1, 0)
     rows_pass(0)
-    rows_pass(1)
+    sum_middle(1)
+    scatter_finish(1)
+    step_c(1, 0)
 
     def left_panel(m, carry):
         rows = pl.ds(pl.multiple_of(m * 256, 256), 256)
@@ -415,6 +418,9 @@
         return carry
 
     lax.fori_loop(0, 4, left_panel, 0)
+    sum_gather(1)
+    step_a(1, 1)
+    rows_pass(1)
     step_b(1, 1)
     step_c(1, 1)
     rows_finish(0)
@@ -449,6 +455,7 @@
     slices = pltpu.VMEM((2, 4, 32, 256), F32)
     square = pltpu.VMEM((256, 256), F32)
     left = pltpu.VMEM((1024, 512), BF16)
+    columns = pltpu.VMEM((2, 8, 32, 128), F32)
     return pl.pallas_call(
         exchange_kernel,
         out_shape=jax.ShapeDtypeStruct(trailing.shape, F32),
@@ -464,7 +471,7 @@
             pltpu.VMEM((256, 1024), F32),
             by_rows, pieces, pieces, by_rows, halves, halves, halves,
             pltpu.VMEM((2, 128, 128), F32),
-            by_rows, whole, pltpu.VMEM((8, 32, 256), F32), slices, slices, whole,
+            by_rows, pltpu.VMEM((8, 32, 256), F32), columns, columns, slices, slices, whole,
             square, square, square, left, left,
             dma((8,)),
             dma((2, 2)),
@@ -479,8 +486,8 @@
             dma((2, 4)),
             dma((2,)),
             dma((2,)),
-            dma((7,)),
-            dma((8,)),
+            dma((2, 7)),
+            dma((2, 8)),
             dma((2, 3)),
             dma((2, 4)),
             dma((2, 3)),

time: 95 us -> 97 us (1.021)
  Pallas kernels: 90.2 us -> 92.3 us
    pallas_call x1, Pallas kernels: 90.2 us -> 92.3 us  [exchange(): pl.pallas_call(exchange_kernel, out_shape=jax.ShapeDtypeStruct(trailing.s...]
where the time goes in v4:
time: 97 us; the launch traced here: 96.9 us
  Pallas kernels  92.3 us (95%)
  local copies, waits for them, and re-layouts  4.62 us (5%)
    pallas_call x1, Pallas kernels, exchange(): pl.pallas_call(exchange_kernel, out_shape=jax.ShapeDtypeStruct(trailing.s...  92.3 us
    unnamed x3, local copies, waits for them, and re-layouts  4.62 us

profile of v4, /device:TPU:1, one launch (start us, length us, event | category | flops | bytes accessed | tf_op | source)
XLA Modules:
  0.0 96.9 jit_solution(13219208725075949439)
XLA Ops:
  0.0 0.0 copy-start
  0.0 1.2 %copy-done = f32[4,1024,64]{1,2,0:T(8,128)S(1)} copy-done((f32[4,1024,64]{1,2,0:T(8,128)S(1)}, f32[4,1024,64]{1,2,0:T(8,128)}, u32[]{:S(2)}) %copy-start) | copy-done | bytes 1048600
  1.2 92.3 %exchange.1 = f32[1024,2048]{1,0:T(8,128)S(1)} custom-call(f32[1024,2048]{1,0:T(8,128)} %a_hbm.1, f32[256,1024]{1,0:T(8,128)S(1)} %bitcast.3), custom_call_target="tpu_custom_call" | custom-call | flops 8000000000 | bytes 16777216 | tf_op jit(solution)/shard_map/exchange/pallas_call | solution.py:459
  93.5 3.4 %copy.4 = f32[1024,2048]{1,0:T(8,128)} copy(f32[1024,2048]{1,0:T(8,128)S(1)} %exchange.1) | data formatting | bytes 16777216
Async XLA Ops:
  0.0 1.2 %copy-start = (f32[4,1024,64]{1,2,0:T(8,128)S(1)}, f32[4,1024,64]{1,2,0:T(8,128)}, u32[]{:S(2)}) copy-start(f32[4,1024,64]{1,2,0:T(8,128)} %param.3) | copy-start | bytes 3145732

commit v5 on v4

--- a/solution.py
+++ b/solution.py
@@ -34,7 +34,7 @@
     a_hbm, raw_ref,
     out_ref,
     a_buf, a_hi, a_lo, vt, vr, vc, yc, yp, drx, yh, zrx, ys, yr,
-    pb, sb, cb, xb, yb, gb, pw, inv, mm, lhi_ref, llo_ref,
+    pb, sb, cb, xb, yb, gb, pw, inv, tm, lhi_ref, llo_ref, vhi_ref, vlo_ref,
     a_sem,
     t_send, t_recv, p_send, p_recv,
     d_send, d_recv, zr_send, zr_recv, za_send, za_recv, e_send, e_recv,
@@ -329,28 +329,48 @@
         jp = h * (n - 1) + (1 - h) * ((y // 2 + n // 3) % 2)
         return b, h, jp
 
+    def pair(ref, here):
+        return jnp.concatenate(
+            [ref[(0,) + here].reshape(256, 128), ref[(1,) + here].reshape(256, 128)], axis=1
+        )
+
+    def subtract(i, high_ref, low_ref, right, store):
+        high, low = split(right)
+        right = jnp.concatenate([high, low, high], axis=1)
+
+        def tile(m, inside):
+            rows = pl.ds(pl.multiple_of(m * 512, 512), 512)
+            left_high = high_ref[rows]
+            left = jnp.concatenate([left_high, left_high, low_ref[rows]], axis=1)
+            store(rows, a_buf[i, rows] - quick(left, right, NT))
+            return inside
+
+        lax.fori_loop(0, 2, tile, 0)
+
+    def begin(i, carry):
+        here = (i // 4, i // 2 % 2, pl.ds(2 * (i % 2), 2))
+
+        def store(rows, value):
+            a_buf[i, rows] = value
+
+        subtract(i, lhi_ref, llo_ref, pair(vc, here), store)
+        return carry
+
     def finish(t, carry):
         b, h, jp = place(t)
         for q in range(2):
             for n in range(2):
                 step_d(1, q, b, h, 2 * jp + n)
         here = (b, h, pl.ds(2 * jp, 2))
-        right = jnp.concatenate(
-            [ref[(q,) + here].reshape(256, 128) for ref in (yc, vc) for q in range(2)], axis=1
-        )
-        high, low = split(right)
-        right = jnp.concatenate([high, low, high], axis=1)
         i = b * 4 + h * 2 + jp
-
-        def tile(m, inside):
-            rows = pl.ds(pl.multiple_of(m * 512, 512), 512)
-            left_high = lhi_ref[rows]
-            left = jnp.concatenate([left_high, left_high, llo_ref[rows]], axis=1)
-            columns = pl.ds(pl.multiple_of(i * 256, 256), 256)
-            out_ref[rows, columns] = a_buf[i, rows] - quick(left, right, NT)
-            return inside
-
-        lax.fori_loop(0, 2, tile, 0)
+        high, low = split(jnp.concatenate([pair(yc, here), pair(vc, here)], axis=1))
+        total = quick(jnp.concatenate([high, high, low], axis=1), tm[...], NN)
+        columns = pl.ds(pl.multiple_of(i * 256, 256), 256)
+
+        def store(rows, value):
+            out_ref[rows, columns] = value
+
+        subtract(i, vhi_ref, vlo_ref, total, store)
         return carry
 
     t_start(0, 0)
@@ -359,6 +379,7 @@
     xb[0, x] = pb[col]
     sum_start(0)
     step_a(0, 0)
+    sum_middle(0)
 
     for i in range(8):
         slab(i).wait()
@@ -371,72 +392,82 @@
             return carry
 
         lax.fori_loop(0, 8, chop, 0)
-    step_b(0, 0)
-    step_c(0, 0)
+        if i == 3:
+            step_b(0, 0)
+            step_c(0, 0)
     step_a(0, 1)
-    sum_middle(0)
-    for t in range(4):
-        multiply(0, t)
-        if t == 1:
-            step_b(0, 1)
-            step_c(0, 1)
-            sum_gather(0)
+    multiply(0, 0)
+    multiply(0, 1)
+    step_b(0, 1)
+    step_c(0, 1)
+    multiply(0, 2)
+    multiply(0, 3)
     pair_start(0)
+    sum_gather(0)
     inner(sb.at[0], product_rows(0))
     scatter_start(0)
     column_start(0)
+    multiply(1, 0)
     sum_finish(0)
     factor_start()
     lax.fori_loop(0, 5, factor_double, 0)
-    multiply(1, 0)
+    scatter_finish(0)
+    multiply(1, 1)
+    multiply(1, 2)
+    multiply(1, 3)
+    pair_start(1)
+    inner(sb.at[1], product_rows(1))
+    scatter_start(1)
+    column_start(1)
+    step_a(1, 0)
     factor_scale()
     factor_join(64)
     factor_join(128)
-    multiply(1, 1)
-    scatter_finish(0)
-    multiply(1, 2)
     column_finish(0)
-    multiply(1, 3)
-    pair_start(1)
-    inner(sb.at[1], product_rows(1))
-    column_start(1)
-    scatter_start(1)
-    step_a(1, 0)
+    scatter_finish(1)
     column_finish(1)
     sum_start(1)
     step_b(1, 0)
     rows_pass(0)
+
+    def split_rows(m, carry):
+        rows = pl.ds(pl.multiple_of(m * 256, 256), 256)
+        high, low = split(own_rows(vr, m))
+        vhi_ref[rows] = high
+        vlo_ref[rows] = low
+        return carry
+
+    lax.fori_loop(0, 4, split_rows, 0)
     sum_middle(1)
-    scatter_finish(1)
+    step_a(1, 1)
     step_c(1, 0)
-
-    def left_panel(m, carry):
-        rows = pl.ds(pl.multiple_of(m * 256, 256), 256)
-        high, low = split(exact(own_rows(vr, m), inv[...], NT))
-        lhi_ref[rows, :256] = high
-        llo_ref[rows, :256] = low
-        return carry
-
-    lax.fori_loop(0, 4, left_panel, 0)
+    rows_pass(1)
+    rows_finish(0)
     sum_gather(1)
-    step_a(1, 1)
-    rows_pass(1)
     step_b(1, 1)
     step_c(1, 1)
-    rows_finish(0)
     rows_finish(1)
-    sum_finish(1)
-    mm[...] = exact(inv[...].T, exact(gb[1].reshape(256, 256), inv[...], NN), NN)
 
     def left_update(m, carry):
         rows = pl.ds(pl.multiple_of(m * 256, 256), 256)
-        other = exact(own_rows(yr, m), inv[...], NN) - exact(own_rows(vr, m), mm[...], NN)
-        high, low = split(other)
-        lhi_ref[rows, 256:] = high
-        llo_ref[rows, 256:] = low
+        high, low = split(exact(own_rows(yr, m), inv[...], NN))
+        lhi_ref[rows] = high
+        llo_ref[rows] = low
         return carry
 
     lax.fori_loop(0, 4, left_update, 0)
+    lax.fori_loop(0, 8, begin, 0)
+    sum_finish(1)
+    inner_factor = inv[...]
+    coupling = exact(inner_factor.T, exact(gb[1].reshape(256, 256), inner_factor, NN), NN)
+    high, low = split(inner_factor)
+    tm[0:256] = high
+    tm[512:768] = low
+    tm[1024:1280] = high
+    high, low = split(-coupling)
+    tm[256:512] = high
+    tm[768:1024] = low
+    tm[1280:1536] = high
     lax.fori_loop(0, 8, finish, 0)
 
     for copy, cond in sent:
@@ -454,7 +485,7 @@
     whole = pltpu.VMEM((2, 8, 32, 256), F32)
     slices = pltpu.VMEM((2, 4, 32, 256), F32)
     square = pltpu.VMEM((256, 256), F32)
-    left = pltpu.VMEM((1024, 512), BF16)
+    left = pltpu.VMEM((1024, 256), BF16)
     columns = pltpu.VMEM((2, 8, 32, 128), F32)
     return pl.pallas_call(
         exchange_kernel,
@@ -472,7 +503,7 @@
             by_rows, pieces, pieces, by_rows, halves, halves, halves,
             pltpu.VMEM((2, 128, 128), F32),
             by_rows, pltpu.VMEM((8, 32, 256), F32), columns, columns, slices, slices, whole,
-            square, square, square, left, left,
+            square, square, pltpu.VMEM((1536, 256), BF16), left, left, left, left,
             dma((8,)),
             dma((2, 2)),
             dma((2, 2, 2)),

time: 97 us -> 92.4 us (0.953)
  the two profiles are of different devices: /device:TPU:1 before, /device:TPU:0 now
where the time goes in v5:
time: 92.4 us; the launch traced here: 92 us
  Pallas kernels  87.4 us (95%)
  local copies, waits for them, and re-layouts  4.62 us (5%)
    pallas_call x1, Pallas kernels, exchange(): pl.pallas_call(exchange_kernel, out_shape=jax.ShapeDtypeStruct(trailing.s...  87.4 us
    unnamed x3, local copies, waits for them, and re-layouts  4.62 us

profile of v5, /device:TPU:0, one launch (start us, length us, event | category | flops | bytes accessed | tf_op | source)
XLA Modules:
  0.0 92.0 jit_solution(13789266911912315018)
XLA Ops:
  0.0 0.0 copy-start
  0.0 1.2 %copy-done = f32[4,1024,64]{1,2,0:T(8,128)S(1)} copy-done((f32[4,1024,64]{1,2,0:T(8,128)S(1)}, f32[4,1024,64]{1,2,0:T(8,128)}, u32[]{:S(2)}) %copy-start) | copy-done | bytes 1048600
  1.2 87.4 %exchange.1 = f32[1024,2048]{1,0:T(8,128)S(1)} custom-call(f32[1024,2048]{1,0:T(8,128)} %a_hbm.1, f32[256,1024]{1,0:T(8,128)S(1)} %bitcast.3), custom_call_target="tpu_custom_call" | custom-call | flops 8000000000 | bytes 16777216 | tf_op jit(solution)/shard_map/exchange/pallas_call | solution.py:490
  88.6 3.4 %copy.4 = f32[1024,2048]{1,0:T(8,128)} copy(f32[1024,2048]{1,0:T(8,128)S(1)} %exchange.1) | data formatting | bytes 16777216
Async XLA Ops:
  0.0 1.2 %copy-start = (f32[4,1024,64]{1,2,0:T(8,128)S(1)}, f32[4,1024,64]{1,2,0:T(8,128)}, u32[]{:S(2)}) copy-start(f32[4,1024,64]{1,2,0:T(8,128)} %param.3) | copy-start | bytes 3145732

commit v6 on v5

--- a/solution.py
+++ b/solution.py
@@ -85,7 +85,8 @@
 
     for d in range(1, 4):
         greet(dev((x + d) % 4, y, z, k))
-        greet(dev(x, (y + d) % 4, z, k))
+        greet(dev(x, (y + d) % 4, z, 0))
+        greet(dev(x, (y + d) % 4, z, 1))
     for d in range(1, 8):
         greet((row, (col + d) % 8))
 
@@ -104,23 +105,31 @@
             vt[q * 128:(q + 1) * 128, n * 128:(n + 1) * 128] = piece
             vr[q, n // 4, n % 4] = piece.T
 
-    pl.semaphore_wait(barrier, jnp.where(y != z, 15, 13))
-
-    def t_start(ph, q):
-        target = vc if ph == 0 else yc
-        source = vr.at[q, k, z] if ph == 0 else ys.at[q]
-        place = target.at[q, b_own, k, z]
+    pl.semaphore_wait(barrier, jnp.where(y != z, 18, 16))
+
+    def panel_start(q):
+        for d in range(4):
+            j = (y + d) % 4
+            send(
+                copy_to(vr.at[q, k, j], vc.at[q, b_own, k, j], t_send.at[0, q, d],
+                        t_recv.at[0, q, k], dev(x, j, z, x // 2)),
+                y == z if d else jnp.logical_and(y == z, jnp.logical_not(is_src)),
+            )
+
+        @pl.when(stays)
+        def _():
+            vc[q, b_own, k, y] = vr[q, k, y]
+
+    def product_start(q):
         send(
-            copy_to(source, place, t_send.at[ph, q], t_recv.at[ph, q, k], dev(x, z, y, x // 2)),
+            copy_to(ys.at[q], yc.at[q, b_own, k, z], t_send.at[1, q, 0], t_recv.at[1, q, k],
+                    dev(x, z, y, x // 2)),
             jnp.logical_not(stays),
         )
 
         @pl.when(stays)
         def _():
-            if ph == 0:
-                vc[q, b_own, k, z] = vr[q, k, z]
-            else:
-                yc[q, b_own, k, z] = ys[q]
+            yc[q, b_own, k, z] = ys[q]
 
     def spread(ph, q, slot, b, h, j, along_x, cond):
         piece = (vc if ph == 0 else yc).at[q, b, h, j]
@@ -207,7 +216,7 @@
         total = zrx[q, 0] + zrx[q, 1] + zrx[q, 2] + zrx[q, 3]
         ys[q] = total
         yr[q, k, z] = total
-        t_start(1, q)
+        product_start(q)
         for d in range(1, 4):
             send(copy_to(ys.at[q], yr.at[q, k, z], za_send.at[q, d - 1], za_recv.at[q, z],
                          dev(x, y, (z + d) % 4, k)))
@@ -338,20 +347,15 @@
         high, low = split(right)
         right = jnp.concatenate([high, low, high], axis=1)
 
-        def tile(m, inside):
-            rows = pl.ds(pl.multiple_of(m * 512, 512), 512)
-            left_high = high_ref[rows]
-            left = jnp.concatenate([left_high, left_high, low_ref[rows]], axis=1)
-            store(rows, a_buf[i, rows] - quick(left, right, NT))
-            return inside
-
-        lax.fori_loop(0, 2, tile, 0)
+        left_high = high_ref[...]
+        left = jnp.concatenate([left_high, left_high, low_ref[...]], axis=1)
+        store(a_buf[i] - quick(left, right, NT))
 
     def begin(i, carry):
         here = (i // 4, i // 2 % 2, pl.ds(2 * (i % 2), 2))
 
-        def store(rows, value):
-            a_buf[i, rows] = value
+        def store(value):
+            a_buf[i] = value
 
         subtract(i, lhi_ref, llo_ref, pair(vc, here), store)
         return carry
@@ -367,14 +371,14 @@
         total = quick(jnp.concatenate([high, high, low], axis=1), tm[...], NN)
         columns = pl.ds(pl.multiple_of(i * 256, 256), 256)
 
-        def store(rows, value):
-            out_ref[rows, columns] = value
+        def store(value):
+            out_ref[:, columns] = value
 
         subtract(i, vhi_ref, vlo_ref, total, store)
         return carry
 
-    t_start(0, 0)
-    t_start(0, 1)
+    panel_start(0)
+    panel_start(1)
     inner(pb, lambda m: own_rows(vr, m))
     xb[0, x] = pb[col]
     sum_start(0)
@@ -408,11 +412,8 @@
     scatter_start(0)
     column_start(0)
     multiply(1, 0)
-    sum_finish(0)
-    factor_start()
-    lax.fori_loop(0, 5, factor_double, 0)
+    multiply(1, 1)
     scatter_finish(0)
-    multiply(1, 1)
     multiply(1, 2)
     multiply(1, 3)
     pair_start(1)
@@ -420,15 +421,15 @@
     scatter_start(1)
     column_start(1)
     step_a(1, 0)
-    factor_scale()
-    factor_join(64)
-    factor_join(128)
+    sum_finish(0)
+    factor_start()
     column_finish(0)
     scatter_finish(1)
     column_finish(1)
     sum_start(1)
     step_b(1, 0)
     rows_pass(0)
+    lax.fori_loop(0, 5, factor_double, 0)
 
     def split_rows(m, carry):
         rows = pl.ds(pl.multiple_of(m * 256, 256), 256)
@@ -437,12 +438,15 @@
         vlo_ref[rows] = low
         return carry
 
-    lax.fori_loop(0, 4, split_rows, 0)
     sum_middle(1)
     step_a(1, 1)
     step_c(1, 0)
     rows_pass(1)
     rows_finish(0)
+    lax.fori_loop(0, 4, split_rows, 0)
+    factor_scale()
+    factor_join(64)
+    factor_join(128)
     sum_gather(1)
     step_b(1, 1)
     step_c(1, 1)
@@ -505,7 +509,7 @@
             by_rows, pltpu.VMEM((8, 32, 256), F32), columns, columns, slices, slices, whole,
             square, square, pltpu.VMEM((1536, 256), BF16), left, left, left, left,
             dma((8,)),
-            dma((2, 2)),
+            dma((2, 2, 4)),
             dma((2, 2, 2)),
             dma((2, 2, 9, 3)),
             dma((2, 2, 2, 2, 4)),

time: 92.4 us -> 88.7 us (0.960)
  Pallas kernels: 87.4 us -> 83.9 us
    pallas_call x1, Pallas kernels: 87.4 us -> 83.9 us  [exchange(): pl.pallas_call(exchange_kernel, out_shape=jax.ShapeDtypeStruct(trailing.s...]
where the time goes in v6:
time: 88.7 us; the launch traced here: 88.6 us
  Pallas kernels  83.9 us (95%)
  local copies, waits for them, and re-layouts  4.62 us (5%)
    pallas_call x1, Pallas kernels, exchange(): pl.pallas_call(exchange_kernel, out_shape=jax.ShapeDtypeStruct(trailing.s...  83.9 us
    unnamed x3, local copies, waits for them, and re-layouts  4.62 us

profile of v6, /device:TPU:0, one launch (start us, length us, event | category | flops | bytes accessed | tf_op | source)
XLA Modules:
  0.0 88.6 jit_solution(14702242731667373886)
XLA Ops:
  0.0 0.0 copy-start
  0.0 1.2 %copy-done = f32[4,1024,64]{1,2,0:T(8,128)S(1)} copy-done((f32[4,1024,64]{1,2,0:T(8,128)S(1)}, f32[4,1024,64]{1,2,0:T(8,128)}, u32[]{:S(2)}) %copy-start) | copy-done | bytes 1048600
  1.2 83.9 %exchange.1 = f32[1024,2048]{1,0:T(8,128)S(1)} custom-call(f32[1024,2048]{1,0:T(8,128)} %a_hbm.1, f32[256,1024]{1,0:T(8,128)S(1)} %bitcast.3), custom_call_target="tpu_custom_call" | custom-call | flops 8000000000 | bytes 16777216 | tf_op jit(solution)/shard_map/exchange/pallas_call | solution.py:494
  85.2 3.4 %copy.4 = f32[1024,2048]{1,0:T(8,128)} copy(f32[1024,2048]{1,0:T(8,128)S(1)} %exchange.1) | data formatting | bytes 16777216
Async XLA Ops:
  0.0 1.2 %copy-start = (f32[4,1024,64]{1,2,0:T(8,128)S(1)}, f32[4,1024,64]{1,2,0:T(8,128)}, u32[]{:S(2)}) copy-start(f32[4,1024,64]{1,2,0:T(8,128)} %param.3) | copy-start | bytes 3145732

commit v7 on v6

--- a/solution.py
+++ b/solution.py
@@ -430,6 +430,10 @@
     step_b(1, 0)
     rows_pass(0)
     lax.fori_loop(0, 5, factor_double, 0)
+    factor_scale()
+    factor_join(64)
+    factor_join(128)
+    step_a(1, 1)
 
     def split_rows(m, carry):
         rows = pl.ds(pl.multiple_of(m * 256, 256), 256)
@@ -439,17 +443,13 @@
         return carry
 
     sum_middle(1)
-    step_a(1, 1)
     step_c(1, 0)
     rows_pass(1)
     rows_finish(0)
     lax.fori_loop(0, 4, split_rows, 0)
-    factor_scale()
-    factor_join(64)
-    factor_join(128)
-    sum_gather(1)
     step_b(1, 1)
     step_c(1, 1)
+    sum_gather(1)
     rows_finish(1)
 
     def left_update(m, carry):

time: 88.7 us -> 92.5 us (1.043); the launches traced: 88.6 us -> 91.4 us
  Pallas kernels: 83.9 us -> 86.7 us
    pallas_call x1, Pallas kernels: 83.9 us -> 86.7 us  [exchange(): pl.pallas_call(exchange_kernel, out_shape=jax.ShapeDtypeStruct(trailing.s...]
where the time goes in v7:
time: 92.5 us; the launch traced here: 91.4 us
  Pallas kernels  86.7 us (94%)
  local copies, waits for them, and re-layouts  4.62 us (5%)
    pallas_call x1, Pallas kernels, exchange(): pl.pallas_call(exchange_kernel, out_shape=jax.ShapeDtypeStruct(trailing.s...  86.7 us
    unnamed x3, local copies, waits for them, and re-layouts  4.62 us

profile of v7, /device:TPU:0, one launch (start us, length us, event | category | flops | bytes accessed | tf_op | source)
XLA Modules:
  0.0 91.4 jit_solution(1952942978383074009)
XLA Ops:
  0.0 0.0 copy-start
  0.0 1.2 %copy-done = f32[4,1024,64]{1,2,0:T(8,128)S(1)} copy-done((f32[4,1024,64]{1,2,0:T(8,128)S(1)}, f32[4,1024,64]{1,2,0:T(8,128)}, u32[]{:S(2)}) %copy-start) | copy-done | bytes 1048600
  1.2 86.7 %exchange.1 = f32[1024,2048]{1,0:T(8,128)S(1)} custom-call(f32[1024,2048]{1,0:T(8,128)} %a_hbm.1, f32[256,1024]{1,0:T(8,128)S(1)} %bitcast.3), custom_call_target="tpu_custom_call" | custom-call | flops 8000000000 | bytes 16777216 | tf_op jit(solution)/shard_map/exchange/pallas_call | solution.py:494
  88.0 3.4 %copy.4 = f32[1024,2048]{1,0:T(8,128)} copy(f32[1024,2048]{1,0:T(8,128)S(1)} %exchange.1) | data formatting | bytes 16777216
Async XLA Ops:
  0.0 1.2 %copy-start = (f32[4,1024,64]{1,2,0:T(8,128)S(1)}, f32[4,1024,64]{1,2,0:T(8,128)}, u32[]{:S(2)}) copy-start(f32[4,1024,64]{1,2,0:T(8,128)} %param.3) | copy-start | bytes 3145732

commit v8 on v6

--- a/solution.py
+++ b/solution.py
@@ -418,15 +418,15 @@
     multiply(1, 3)
     pair_start(1)
     inner(sb.at[1], product_rows(1))
+    column_start(1)
     scatter_start(1)
-    column_start(1)
     step_a(1, 0)
     sum_finish(0)
     factor_start()
     column_finish(0)
-    scatter_finish(1)
     column_finish(1)
     sum_start(1)
+    scatter_finish(1)
     step_b(1, 0)
     rows_pass(0)
     lax.fori_loop(0, 5, factor_double, 0)

time: 88.7 us -> 86 us (0.970)
  Pallas kernels: 83.9 us -> 81.3 us
    pallas_call x1, Pallas kernels: 83.9 us -> 81.3 us  [exchange(): pl.pallas_call(exchange_kernel, out_shape=jax.ShapeDtypeStruct(trailing.s...]
where the time goes in v8:
time: 86 us; the launch traced here: 85.9 us
  Pallas kernels  81.3 us (95%)
  local copies, waits for them, and re-layouts  4.62 us (5%)
    pallas_call x1, Pallas kernels, exchange(): pl.pallas_call(exchange_kernel, out_shape=jax.ShapeDtypeStruct(trailing.s...  81.3 us
    unnamed x3, local copies, waits for them, and re-layouts  4.62 us

profile of v8, /device:TPU:0, one launch (start us, length us, event | category | flops | bytes accessed | tf_op | source)
XLA Modules:
  0.0 85.9 jit_solution(499037563202266625)
XLA Ops:
  0.0 0.0 copy-start
  0.0 1.2 %copy-done = f32[4,1024,64]{1,2,0:T(8,128)S(1)} copy-done((f32[4,1024,64]{1,2,0:T(8,128)S(1)}, f32[4,1024,64]{1,2,0:T(8,128)}, u32[]{:S(2)}) %copy-start) | copy-done | bytes 1048600
  1.2 81.3 %exchange.1 = f32[1024,2048]{1,0:T(8,128)S(1)} custom-call(f32[1024,2048]{1,0:T(8,128)} %a_hbm.1, f32[256,1024]{1,0:T(8,128)S(1)} %bitcast.3), custom_call_target="tpu_custom_call" | custom-call | flops 8000000000 | bytes 16777216 | tf_op jit(solution)/shard_map/exchange/pallas_call | solution.py:494
  82.5 3.4 %copy.4 = f32[1024,2048]{1,0:T(8,128)} copy(f32[1024,2048]{1,0:T(8,128)S(1)} %exchange.1) | data formatting | bytes 16777216
Async XLA Ops:
  0.0 1.2 %copy-start = (f32[4,1024,64]{1,2,0:T(8,128)S(1)}, f32[4,1024,64]{1,2,0:T(8,128)}, u32[]{:S(2)}) copy-start(f32[4,1024,64]{1,2,0:T(8,128)} %param.3) | copy-start | bytes 3145732
